TPU v7x, 128 devices: a whole 4x4x4 slice. The times are simulated.
128 devices in a mesh: gx: 16 (over z, x), yz: 8 (over y, core).
Axes of the slice: x: 4, y: 4, z: 4, core: 2. Of those that a mesh axis runs over, the one named last changes fastest.
Arguments:
- populations: float32 [19, 128, 64, 128], P(None, 'gx', 'yz'), may hold values from 0.02 to 0.1
- cell_grain: int32 [128, 64, 128], P('gx', 'yz'), may hold values from -1 to 1023, as said below
- near_rows: int32 [128, 1024], P(('gx', 'yz')), may hold values from -1 to 511, as said below
- contact_pairs: int32 [2, 131072], P(None, ('gx', 'yz')), may hold values from 0 to 1023, as said below
- grain_position: float32 [3, 65536], P(None, ('gx', 'yz')), may hold values from 0 to 6
- grain_velocity: float32 [3, 65536], P(None, ('gx', 'yz')), may hold values from -0.1 to 0.1
- grain_radius: float32 [65536], P(('gx', 'yz')), may hold values from 0.8 to 1.6
- grain_mass: float32 [65536], P(('gx', 'yz')), may hold values from 2 to 20
Outputs:
- populations_next: float32 [19, 128, 64, 128], P(None, 'gx', 'yz')
- velocity_next: float32 [3, 65536], P(None, ('gx', 'yz'))
- position_next: float32 [3, 65536], P(None, ('gx', 'yz'))
Inputs may be any that keep to these rules, and one draw needn't show every extreme that they name: `near_rows`: entry o * 8 + s of device d's row names a row of device o's grains or is -1; in each block of 8 entries the live ones come first, are distinct, and number 1 to 8; every device has one block with all 8 live. `cell_grain`: A solid cell names a live entry of the list of the device whose brick holds it; the share of solid cells differs from brick to brick. `contact_pairs`: column p belongs to device p // 1024: its first row is a row of that device's grains, its second a live entry of that device's list.
All inputs are finite; a program needn't handle non-finite values.
Results may differ from a plain program's by a relative error of at most 0.0003.
Values sent between devices are 32-bit elements; how exact they have to be, the bound alone decides.
No kernel may reach another device: no remote copies, remote signals or barrier semaphores. Data moves between devices by JAX's collectives and lax.ppermute only.
A program may use at most 64 MiB of HBM per device.

v0:
```python
import math

import jax
import jax.numpy as jnp
import numpy as np
from jax import lax
from jax.sharding import PartitionSpec as P

lattice_dirs = (
    (0, 0, 0),
    (1, 0, 0),
    (-1, 0, 0),
    (0, 1, 0),
    (0, -1, 0),
    (0, 0, 1),
    (0, 0, -1),
    (1, 1, 0),
    (-1, -1, 0),
    (1, -1, 0),
    (-1, 1, 0),
    (1, 0, 1),
    (-1, 0, -1),
    (1, 0, -1),
    (-1, 0, 1),
    (0, 1, 1),
    (0, -1, -1),
    (0, 1, -1),
    (0, -1, 1),
)
lattice_weights = (1.0 / 3.0,) + (1.0 / 18.0,) * 6 + (1.0 / 36.0,) * 12
opposite = (0, 2, 1, 4, 3, 6, 5, 8, 7, 10, 9, 12, 11, 14, 13, 16, 15, 18, 17)
relax_rate = 1.25
stiffness = 0.5
damping = 0.5
highest = lax.Precision.HIGHEST


def extended(block, sides, width):
    for axis, dim in sides:
        count = lax.axis_size(axis)
        forward = [(i, i + 1) for i in range(count - 1)]
        forward.append((count - 1, 0))
        backward = [(target, source) for source, target in forward]
        low = lax.ppermute(
            lax.slice_in_dim(block, block.shape[dim] - width, None, axis=dim), axis, forward
        )
        high = lax.ppermute(lax.slice_in_dim(block, 0, width, axis=dim), axis, backward)
        block = jnp.concatenate([low, block, high], axis=dim)
    return block


def project(direction, parts):
    total = None
    for compo in range(3):
        factor = lattice_dirs[direction][compo]
        if factor != 0:
            term = factor * parts[compo]
            total = term if total is None else total + term
    return total


def indicator(ids, count):
    return (ids[..., None] == jnp.arange(count, dtype=jnp.int32)).astype(jnp.float32)


def collide(populations):
    vectors = jnp.asarray(np.array(lattice_dirs, np.float32))
    weights = jnp.asarray(np.array(lattice_weights, np.float32))[:, None, None, None]
    density = jnp.sum(populations, axis=0)
    speeds = jnp.einsum("ic,ixyz->cxyz", vectors, populations, precision=highest) / density[None]
    square = jnp.sum(speeds * speeds, axis=0)
    along = jnp.einsum("ic,cxyz->ixyz", vectors, speeds, precision=highest)
    equil = weights * density[None] * (1.0 + 3.0 * along + 4.5 * along * along - 1.5 * square[None])
    return populations + relax_rate * (equil - populations)


def stream_force(populations, fluid, padded):
    width_x = populations.shape[1]
    width_y = populations.shape[2]

    def shifted(low, high, shift_x, shift_y, shift_z):
        piece = padded[
            low:high, 1 - shift_x : 1 - shift_x + width_x, 1 - shift_y : 1 - shift_y + width_y
        ]
        if shift_z != 0:
            piece = jnp.roll(piece, shift_z, axis=3)
        return piece

    here = shifted(0, 24, 0, 0, 0)
    fresh = [here[0]]
    force = [jnp.zeros_like(here[0]) for compo in range(3)]
    for direction in range(1, 19):
        shift_x, shift_y, shift_z = lattice_dirs[direction]
        back = opposite[direction]
        weight = lattice_weights[direction]
        source_pop = shifted(direction, direction + 1, shift_x, shift_y, shift_z)[0]
        source_aux = shifted(19, 23, shift_x, shift_y, shift_z)
        bounce = here[back] + 6.0 * weight * here[23] * project(direction, source_aux[0:3])
        fresh.append(source_aux[3] * source_pop + (1.0 - source_aux[3]) * bounce)
        target_pop = shifted(back, back + 1, -shift_x, -shift_y, -shift_z)[0]
        target_aux = shifted(22, 24, -shift_x, -shift_y, -shift_z)
        link = (
            target_aux[0]
            * (2.0 * target_pop + 6.0 * weight * target_aux[1] * project(direction, here[19:22]))
            * (1.0 - here[22])
        )
        for compo in range(3):
            factor = lattice_dirs[direction][compo]
            if factor != 0:
                force[compo] = force[compo] - factor * link
    read = jnp.where(fluid[None], jnp.stack(fresh), populations)
    return (read, jnp.stack(force))


def contact_force(pos_a, vel_a, rad_a, pos_b, vel_b, rad_b):
    offset = pos_a - pos_b
    length = jnp.sqrt(jnp.sum(offset * offset, axis=0))
    normal = offset / jnp.maximum(length, 1.0)
    intersection = jnp.maximum(rad_a + rad_b - length, 0.0)
    closing = jnp.sum((vel_a - vel_b) * normal, axis=0)
    return (stiffness * intersection - damping * intersection * closing) * normal


def local(
    populations,
    cell_grain,
    near_rows,
    contact_pairs,
    grain_position,
    grain_velocity,
    grain_radius,
    grain_mass,
):
    devices = lax.axis_size(("gx", "yz"))
    near_count = near_rows.shape[1]
    slot_count = near_count // devices
    owned = grain_position.shape[1]
    width_x = populations.shape[1]
    width_y = populations.shape[2]
    depth = populations.shape[3]
    plane = width_y * depth
    local_state = jnp.concatenate([grain_position, grain_velocity, grain_radius[None]], 0)
    asked = lax.all_to_all(
        near_rows.reshape(devices, slot_count),
        ("gx", "yz"),
        split_axis=0,
        concat_axis=0,
        tiled=True,
    )
    row_table = indicator(asked, owned)
    answer = jnp.einsum("cg,osg->cos", local_state, row_table, precision=highest)
    near_state = lax.all_to_all(
        answer, ("gx", "yz"), split_axis=1, concat_axis=1, tiled=True
    ).reshape(7, near_count)
    solid = cell_grain >= 0
    plane_ids = cell_grain.reshape(width_x, plane)
    near_wall = near_state[3:6]

    def wall_plane(ids):
        return jnp.einsum("cn,kn->ck", near_wall, indicator(ids, near_count), precision=highest)

    wall = jnp.moveaxis(lax.map(wall_plane, plane_ids), 1, 0).reshape(3, width_x, width_y, depth)
    post = collide(populations)
    table = jnp.concatenate([post, wall, (~solid).astype(jnp.float32)[None]], 0)
    padded = extended(table, (("gx", 1), ("yz", 2)), 1)
    padded = jnp.concatenate([padded, jnp.sum(padded[:19], axis=0)[None]], 0)
    read, cell_force = stream_force(populations, ~solid, padded)
    force_planes = jnp.moveaxis(cell_force.reshape(3, width_x, plane), 1, 0)

    def add_plane(total, inputs):
        ids, forces = inputs
        return (
            total + jnp.einsum("ck,kn->cn", forces, indicator(ids, near_count), precision=highest),
            None,
        )

    slot_force, unused = lax.scan(
        add_plane, jnp.zeros((3, near_count), jnp.float32), (plane_ids, force_planes)
    )
    returned = lax.all_to_all(
        slot_force.reshape(3, devices, slot_count),
        ("gx", "yz"),
        split_axis=1,
        concat_axis=1,
        tiled=True,
    )
    fluid_force = jnp.einsum("cos,osg->cg", returned, row_table, precision=highest)
    pair_count = contact_pairs.shape[1]
    block = math.gcd(pair_count, 1024)
    first_blocks = contact_pairs[0].reshape(pair_count // block, block)
    second_blocks = contact_pairs[1].reshape(pair_count // block, block)

    def add_pairs(total, inputs):
        first, second = inputs
        first_table = indicator(first, owned)
        second_table = indicator(second, near_count)
        state_a = jnp.einsum("cg,pg->cp", local_state, first_table, precision=highest)
        state_b = jnp.einsum("cn,pn->cp", near_state, second_table, precision=highest)
        push = contact_force(
            state_a[0:3], state_a[3:6], state_a[6], state_b[0:3], state_b[3:6], state_b[6]
        )
        return (total + jnp.einsum("cp,pg->cg", push, first_table, precision=highest), None)

    contact_total, unused = lax.scan(
        add_pairs, jnp.zeros((3, owned), jnp.float32), (first_blocks, second_blocks)
    )
    velocity_next = grain_velocity + (fluid_force + contact_total) / grain_mass[None]
    position_next = grain_position + velocity_next
    return (read, velocity_next, position_next)


def solution(mesh):
    return jax.shard_map(
        local,
        mesh=mesh,
        in_specs=(
            P(None, "gx", "yz", None),
            P("gx", "yz", None),
            P(("gx", "yz"), None),
            P(None, ("gx", "yz")),
            P(None, ("gx", "yz")),
            P(None, ("gx", "yz")),
            P(("gx", "yz")),
            P(("gx", "yz")),
        ),
        out_specs=(P(None, "gx", "yz", None), P(None, ("gx", "yz")), P(None, ("gx", "yz"))),
        check_vma=False,
    )
```

profile of v0, /device:TPU:1, one launch (start us, length us, event | category | flops | bytes accessed | tf_op | source)
XLA Modules:
  0.0 117.3 jit_solution(11880410378608324992)
XLA Ops:
  0.7 0.5 broadcast.423
  1.2 1.3 %reduce.3 = s32[1024]{0:T(1024)S(1)} reduce(s32[1,1024]{1,0:T(1,128)} %param.16, s32[]{:T(128)} %broadcast.423), dimensions={0}, to_apply=%param.16.reduce_sub_computation.3 | reduce | bytes 8196 | tf_op args[2]
  2.5 0.7 all_to_all.12
  3.2 11.5 %all-to-all-start = ((s32[128,1,8]{2,1,0:T(1,128)}), s32[128,1,8]{2,1,0:T(1,128)S(1)}, u32[]{:S(2)}, u32[]{:S(2)}) async-start(s32[128,1,8]{2,1,0:T(1,128)} %bitcast.8), calls=%async_computation | async-start | bytes 131072 | tf_op jit(solution)/shard_map/all_to_all | solution.py:143
  14.7 1.1 reduce_sum.49
  15.9 2.0 %multiply_reduce_fusion = (f32[8,8,128]{2,1,0:T(8,128)S(1)}, f32[3,8,8,128]{3,0,2,1:T(4,128)S(1)}) fusion(f32[8,8,128]{2,1,0:T(8,128)S(1)} %reduce_sum.49, f32[19,3,1,1]{0,1,3,2:T(4,128)} %constant.69, f32[19,8,8,128]{3,2,1,0:T(8,128)} %param.14), kind=kOutput, calls=%fused_computation.63 | convolution fusion | flops 5668864 | bytes 786660 | tf_op jit(solution)/shard_map/ic,ixyz->cxyz/dot_general | solution.py:70
  17.9 0.9 fusion.280
  18.8 0.3 fusion.31
  19.1 0.7 fusion.274
  19.8 0.7 fusion.275
  20.5 0.6 convert_bitcast_fusion
  21.1 3.2 %all-to-all-done = s32[128,1,8]{2,1,0:T(1,128)S(1)} async-done(((s32[128,1,8]{2,1,0:T(1,128)}), s32[128,1,8]{2,1,0:T(1,128)S(1)}, u32[]{:S(2)}, u32[]{:S(2)}) %all-to-all-start) | async-done | bytes 4128 | tf_op jit(solution)/shard_map/all_to_all | solution.py:143
  24.4 1.1 fusion.15
  25.5 1.0 copy.70
  26.5 6.6 %all-to-all-start.1 = ((f32[7,128,8]{0,2,1:T(8,128)}), f32[7,128,8]{0,2,1:T(8,128)S(1)}, u32[]{:S(2)}, u32[]{:S(2)}) async-start(f32[7,128,8]{0,2,1:T(8,128)} %copy.70), calls=%async_computation.1 | async-start | bytes 1048576 | tf_op jit(solution)/shard_map/all_to_all | solution.py:152
  33.1 1.1 fusion.13
  34.2 12.4 %all-to-all-done.1 = f32[7,128,8]{0,2,1:T(8,128)S(1)} async-done(((f32[7,128,8]{0,2,1:T(8,128)}), f32[7,128,8]{0,2,1:T(8,128)S(1)}, u32[]{:S(2)}, u32[]{:S(2)}) %all-to-all-start.1) | async-done | bytes 28704 | tf_op jit(solution)/shard_map/all_to_all | solution.py:152
  46.6 0.2 slice_bitcast_fusion
  47.0 16.3 %while.25 = (s32[]{:T(128)}, f32[8,3,1024]{2,1,0:T(4,128)S(1)}, s32[8,1024]{1,0:T(8,128)S(1)}, f32[3,1024]{1,0:T(4,128)S(1)}, s32[]{:T(128)}) while((s32[]{:T(128)}, f32[8,3,1024]{2,1,0:T(4,128)S(1)}, s32[8,1024]{1,0:T(8,128)S(1)}, f32[3,1024]{1,0:T(4,128)S(1)}, s32[]{:T(128)}) %tuple.82), condition=%wide.region_3.4_spmd, body=%wide.region_2.3_spmd.sunk | while | flops 38797312 | bytes 45125 | solution.py:162
  47.0 2.0 %fusion.318 = f32[8,3,1024]{2,1,0:T(4,128)S(1)} fusion(f32[8,3,1024]{2,1,0:T(4,128)S(1)} %get-tuple-element.211, s32[]{:T(128)} %get-tuple-element.210, f32[3,1024]{1,0:T(4,128)S(1)} %get-tuple-element.218, s32[1024]{0:T(1024)S(1)} %bitcast.268), kind=kOutput, calls=%fused_computation.4.clone.1 | convolution fusion | flops 38797312 | bytes 36868 | tf_op jit(solution)/shard_map/while/body/eval_jaxpr/cn,kn->ck/dot_general | solution.py:160
  49.1 2.0 %fusion.318 = f32[8,3,1024]{2,1,0:T(4,128)S(1)} fusion(f32[8,3,1024]{2,1,0:T(4,128)S(1)} %get-tuple-element.211, s32[]{:T(128)} %get-tuple-element.210, f32[3,1024]{1,0:T(4,128)S(1)} %get-tuple-element.218, s32[1024]{0:T(1024)S(1)} %bitcast.268), kind=kOutput, calls=%fused_computation.4.clone.1 | convolution fusion | flops 38797312 | bytes 36868 | tf_op jit(solution)/shard_map/while/body/eval_jaxpr/cn,kn->ck/dot_general | solution.py:160
  51.1 2.0 %fusion.318 = f32[8,3,1024]{2,1,0:T(4,128)S(1)} fusion(f32[8,3,1024]{2,1,0:T(4,128)S(1)} %get-tuple-element.211, s32[]{:T(128)} %get-tuple-element.210, f32[3,1024]{1,0:T(4,128)S(1)} %get-tuple-element.218, s32[1024]{0:T(1024)S(1)} %bitcast.268), kind=kOutput, calls=%fused_computation.4.clone.1 | convolution fusion | flops 38797312 | bytes 36868 | tf_op jit(solution)/shard_map/while/body/eval_jaxpr/cn,kn->ck/dot_general | solution.py:160
  53.1 2.0 %fusion.318 = f32[8,3,1024]{2,1,0:T(4,128)S(1)} fusion(f32[8,3,1024]{2,1,0:T(4,128)S(1)} %get-tuple-element.211, s32[]{:T(128)} %get-tuple-element.210, f32[3,1024]{1,0:T(4,128)S(1)} %get-tuple-element.218, s32[1024]{0:T(1024)S(1)} %bitcast.268), kind=kOutput, calls=%fused_computation.4.clone.1 | convolution fusion | flops 38797312 | bytes 36868 | tf_op jit(solution)/shard_map/while/body/eval_jaxpr/cn,kn->ck/dot_general | solution.py:160
  55.2 2.0 %fusion.318 = f32[8,3,1024]{2,1,0:T(4,128)S(1)} fusion(f32[8,3,1024]{2,1,0:T(4,128)S(1)} %get-tuple-element.211, s32[]{:T(128)} %get-tuple-element.210, f32[3,1024]{1,0:T(4,128)S(1)} %get-tuple-element.218, s32[1024]{0:T(1024)S(1)} %bitcast.268), kind=kOutput, calls=%fused_computation.4.clone.1 | convolution fusion | flops 38797312 | bytes 36868 | tf_op jit(solution)/shard_map/while/body/eval_jaxpr/cn,kn->ck/dot_general | solution.py:160
  57.2 2.0 %fusion.318 = f32[8,3,1024]{2,1,0:T(4,128)S(1)} fusion(f32[8,3,1024]{2,1,0:T(4,128)S(1)} %get-tuple-element.211, s32[]{:T(128)} %get-tuple-element.210, f32[3,1024]{1,0:T(4,128)S(1)} %get-tuple-element.218, s32[1024]{0:T(1024)S(1)} %bitcast.268), kind=kOutput, calls=%fused_computation.4.clone.1 | convolution fusion | flops 38797312 | bytes 36868 | tf_op jit(solution)/shard_map/while/body/eval_jaxpr/cn,kn->ck/dot_general | solution.py:160
  59.2 2.0 %fusion.318 = f32[8,3,1024]{2,1,0:T(4,128)S(1)} fusion(f32[8,3,1024]{2,1,0:T(4,128)S(1)} %get-tuple-element.211, s32[]{:T(128)} %get-tuple-element.210, f32[3,1024]{1,0:T(4,128)S(1)} %get-tuple-element.218, s32[1024]{0:T(1024)S(1)} %bitcast.268), kind=kOutput, calls=%fused_computation.4.clone.1 | convolution fusion | flops 38797312 | bytes 36868 | tf_op jit(solution)/shard_map/while/body/eval_jaxpr/cn,kn->ck/dot_general | solution.py:160
  61.3 2.0 %fusion.318 = f32[8,3,1024]{2,1,0:T(4,128)S(1)} fusion(f32[8,3,1024]{2,1,0:T(4,128)S(1)} %get-tuple-element.211, s32[]{:T(128)} %get-tuple-element.210, f32[3,1024]{1,0:T(4,128)S(1)} %get-tuple-element.218, s32[1024]{0:T(1024)S(1)} %bitcast.268), kind=kOutput, calls=%fused_computation.4.clone.1 | convolution fusion | flops 38797312 | bytes 36868 | tf_op jit(solution)/shard_map/while/body/eval_jaxpr/cn,kn->ck/dot_general | solution.py:160
  63.5 0.8 fusion.33
  64.2 0.7 fusion.34
  65.0 4.7 %collective-permute-start.1 = (f32[23,1,8,128]{3,2,1,0:T(8,128)S(1)}, f32[23,1,8,128]{3,2,1,0:T(8,128)S(1)}, u32[]{:S(2)}, u32[]{:S(2)}) collective-permute-start(f32[23,1,8,128]{3,2,1,0:T(8,128)S(1)} %get-tuple-element.136), channel_id=1, source_target_pairs={{8,0},{16,8},{24,16},{32,24},{40,32},{48,40},{56,48},{64,56},{72,6... | collective-permute-start | bytes 282632 | tf_op jit(solution)/shard_map/ppermute | solution.py:47
  69.7 2.1 %fusion.10 = f32[7,1024]{1,0:T(8,128)S(1)} fusion(s32[1024]{0:T(1024)S(1)} %bitcast.274, f32[7,128,8]{0,2,1:T(8,128)S(1)} %all-to-all-done.1), kind=kOutput, calls=%fused_computation.15 | convolution fusion | flops 89128960 | bytes 61440 | tf_op jit(solution)/shard_map/while/body/eval_jaxpr/cn,pn->cp/dot_general | solution.py:198
  72.1 1.9 %collective-permute-start.2 = (f32[23,10,1,128]{3,2,1,0:T(1,128)S(1)}, f32[23,10,1,128]{3,2,1,0:T(1,128)S(1)}, u32[]{:S(2)}, u32[]{:S(2)}) collective-permute-start(f32[23,10,1,128]{3,2,1,0:T(1,128)S(1)} %get-tuple-element.132), channel_id=1, source_target_pairs={{0,1},{1,2},{2,3},{3,4},{4,5},{5,6},{6,7},{7,0},{8,9},{9,10},{10,1... | collective-permute-start | bytes 353288 | tf_op jit(solution)/shard_map/ppermute | solution.py:44
  74.2 0.8 slice.1276
  74.9 0.7 slice.1277
  75.6 0.8 slice.1279
  76.4 0.7 slice.1280
  77.0 1.6 %collective-permute-done.3 = f32[23,10,1,128]{3,2,1,0:T(1,128)S(1)} collective-permute-done((f32[23,10,1,128]{3,2,1,0:T(1,128)S(1)}, f32[23,10,1,128]{3,2,1,0:T(1,128)S(1)}, u32[]{:S(2)}, u32[]{:S(2)}) %collective-permute-start.3) | collective-permute-done | bytes 117792 | tf_op jit(solution)/shard_map/ppermute | solution.py:47
  78.6 0.4 fusion.16
  79.0 0.4 pad_maximum_fusion
  79.7 0.4 copy-done.16
  80.1 0.2 fusion.64
  80.3 0.3 fusion.77
  80.9 0.5 fusion.89
  81.4 11.9 %while.26 = (s32[]{:T(128)}, f32[3,1024]{1,0:T(4,128)S(1)}, f32[8,3,1024]{2,1,0:T(4,128)S(1)}, s32[8,1024]{1,0:T(8,128)S(1)}, s32[]{:T(128)}, /*index=5*/s32[]{:T(128)}) while((s32[]{:T(128)}, f32[3,1024]{1,0:T(4,128)S(1)}, f32[8,3,1024]{2,1,0:T(4,128)S(1)}, s32[8,1024]{1,0:T(8,128)S(1)}, s32[]{:T(128)}, /*index=5*/s32[]{:T(128)}) %tuple.83), condition=%wide.region_6.7_spmd.clone, body=%wide.region_5.6_spmd.clone.sunk | while | flops 38803456 | bytes 57431 | solution.py:177
  81.5 1.5 %fusion.320 = f32[3,1024]{1,0:T(4,128)S(1)} fusion(s32[1024]{0:T(1024)S(1)} %bitcast.267, f32[3,1024]{1,0:T(4,128)S(1)} %get-tuple-element.227, f32[8,3,1024]{2,1,0:T(4,128)S(1)} %get-tuple-element.234, s32[]{:T(128)} %get-tuple-element.226, pred[]{:T(512)S(6)} %compare.3), kind=kOutput, calls=%fused_computation.9.clone.1 | convolution fusion | flops 38803456 | bytes 49157 | tf_op jit(solution)/shard_map/while/body/eval_jaxpr/ck,kn->cn/dot_general | solution.py:173
  83.0 1.5 %fusion.320 = f32[3,1024]{1,0:T(4,128)S(1)} fusion(s32[1024]{0:T(1024)S(1)} %bitcast.267, f32[3,1024]{1,0:T(4,128)S(1)} %get-tuple-element.227, f32[8,3,1024]{2,1,0:T(4,128)S(1)} %get-tuple-element.234, s32[]{:T(128)} %get-tuple-element.226, pred[]{:T(512)S(6)} %compare.3), kind=kOutput, calls=%fused_computation.9.clone.1 | convolution fusion | flops 38803456 | bytes 49157 | tf_op jit(solution)/shard_map/while/body/eval_jaxpr/ck,kn->cn/dot_general | solution.py:173
  84.4 1.5 %fusion.320 = f32[3,1024]{1,0:T(4,128)S(1)} fusion(s32[1024]{0:T(1024)S(1)} %bitcast.267, f32[3,1024]{1,0:T(4,128)S(1)} %get-tuple-element.227, f32[8,3,1024]{2,1,0:T(4,128)S(1)} %get-tuple-element.234, s32[]{:T(128)} %get-tuple-element.226, pred[]{:T(512)S(6)} %compare.3), kind=kOutput, calls=%fused_computation.9.clone.1 | convolution fusion | flops 38803456 | bytes 49157 | tf_op jit(solution)/shard_map/while/body/eval_jaxpr/ck,kn->cn/dot_general | solution.py:173
  85.9 1.5 %fusion.320 = f32[3,1024]{1,0:T(4,128)S(1)} fusion(s32[1024]{0:T(1024)S(1)} %bitcast.267, f32[3,1024]{1,0:T(4,128)S(1)} %get-tuple-element.227, f32[8,3,1024]{2,1,0:T(4,128)S(1)} %get-tuple-element.234, s32[]{:T(128)} %get-tuple-element.226, pred[]{:T(512)S(6)} %compare.3), kind=kOutput, calls=%fused_computation.9.clone.1 | convolution fusion | flops 38803456 | bytes 49157 | tf_op jit(solution)/shard_map/while/body/eval_jaxpr/ck,kn->cn/dot_general | solution.py:173
  87.4 1.5 %fusion.320 = f32[3,1024]{1,0:T(4,128)S(1)} fusion(s32[1024]{0:T(1024)S(1)} %bitcast.267, f32[3,1024]{1,0:T(4,128)S(1)} %get-tuple-element.227, f32[8,3,1024]{2,1,0:T(4,128)S(1)} %get-tuple-element.234, s32[]{:T(128)} %get-tuple-element.226, pred[]{:T(512)S(6)} %compare.3), kind=kOutput, calls=%fused_computation.9.clone.1 | convolution fusion | flops 38803456 | bytes 49157 | tf_op jit(solution)/shard_map/while/body/eval_jaxpr/ck,kn->cn/dot_general | solution.py:173
  88.9 1.5 %fusion.320 = f32[3,1024]{1,0:T(4,128)S(1)} fusion(s32[1024]{0:T(1024)S(1)} %bitcast.267, f32[3,1024]{1,0:T(4,128)S(1)} %get-tuple-element.227, f32[8,3,1024]{2,1,0:T(4,128)S(1)} %get-tuple-element.234, s32[]{:T(128)} %get-tuple-element.226, pred[]{:T(512)S(6)} %compare.3), kind=kOutput, calls=%fused_computation.9.clone.1 | convolution fusion | flops 38803456 | bytes 49157 | tf_op jit(solution)/shard_map/while/body/eval_jaxpr/ck,kn->cn/dot_general | solution.py:173
  90.4 1.5 %fusion.320 = f32[3,1024]{1,0:T(4,128)S(1)} fusion(s32[1024]{0:T(1024)S(1)} %bitcast.267, f32[3,1024]{1,0:T(4,128)S(1)} %get-tuple-element.227, f32[8,3,1024]{2,1,0:T(4,128)S(1)} %get-tuple-element.234, s32[]{:T(128)} %get-tuple-element.226, pred[]{:T(512)S(6)} %compare.3), kind=kOutput, calls=%fused_computation.9.clone.1 | convolution fusion | flops 38803456 | bytes 49157 | tf_op jit(solution)/shard_map/while/body/eval_jaxpr/ck,kn->cn/dot_general | solution.py:173
  91.9 1.5 %fusion.320 = f32[3,1024]{1,0:T(4,128)S(1)} fusion(s32[1024]{0:T(1024)S(1)} %bitcast.267, f32[3,1024]{1,0:T(4,128)S(1)} %get-tuple-element.227, f32[8,3,1024]{2,1,0:T(4,128)S(1)} %get-tuple-element.234, s32[]{:T(128)} %get-tuple-element.226, pred[]{:T(512)S(6)} %compare.3), kind=kOutput, calls=%fused_computation.9.clone.1 | convolution fusion | flops 38803456 | bytes 49157 | tf_op jit(solution)/shard_map/while/body/eval_jaxpr/ck,kn->cn/dot_general | solution.py:173
  93.5 0.8 copy.76
  94.3 9.5 %all-to-all-start.2 = ((f32[3,128,8]{2,0,1:T(4,128)}), f32[3,128,8]{2,0,1:T(4,128)S(1)}, u32[]{:S(2)}, u32[]{:S(2)}) async-start(f32[3,128,8]{2,0,1:T(4,128)} %copy.76), calls=%async_computation.2 | async-start | bytes 524288 | tf_op jit(solution)/shard_map/all_to_all | solution.py:180
  104.0 0.7 copy-done.2
  105.3 0.7 copy-done.3
  106.6 0.2 constant_dynamic-update-slice_fusion.3
  106.8 0.2 constant_dynamic-update-slice_fusion.2
  107.0 0.2 constant_dynamic-update-slice_fusion.1
  107.3 0.2 constant_dynamic-update-slice_fusion
  107.5 0.9 broadcast_select_fusion
  108.4 6.5 %all-to-all-done.2 = f32[3,128,8]{2,0,1:T(4,128)S(1)} async-done(((f32[3,128,8]{2,0,1:T(4,128)}), f32[3,128,8]{2,0,1:T(4,128)S(1)}, u32[]{:S(2)}, u32[]{:S(2)}) %all-to-all-start.2) | async-done | bytes 12320 | tf_op jit(solution)/shard_map/all_to_all | solution.py:180
  115.0 0.8 fusion.17
  115.8 1.4 %fusion.279 = (f32[3,512]{1,0:T(4,128)}, f32[3,512]{1,0:T(4,128)}) fusion(f32[3,512]{1,0:T(4,128)S(1)} %copy-done.23, f32[3,512]{1,0:T(4,128)S(1)} %copy-done.22, f32[512]{0:T(512)S(1)} %copy-done.25, f32[3,512]{1,0:T(4,128)S(1)} %fusion.17, s32[1024]{0:T(1024)S(1)} %bitcast.273, f32[1024]{0:T(1024)S(1)} %bitcast.271, f32[1024]{0:T(1024)S(1)} %get-tuple-element.150, ...), kind=kOutput, calls=%fused_computation.547 | convolution fusion | flops 19414016 | bytes 83968 | tf_op jit(solution)/shard_map/while/body/eval_jaxpr/cp,pg->cg/dot_general | solution.py:202
  (106 shorter events, 3.3 us)
Async XLA Ops:
  0.6 17.3 %copy-start.20 = (f32[19,3,1,1]{0,1,3,2:T(4,128)S(1)}, f32[19,3,1,1]{0,1,3,2:T(4,128)}, u32[]{:S(2)}) copy-start(f32[19,3,1,1]{0,1,3,2:T(4,128)} %constant.69) | copy-start | bytes 688
  0.6 18.2 %copy-start.21 = (f32[19]{0:T(128)S(1)}, f32[19]{0:T(128)}, u32[]{:S(2)}) copy-start(f32[19]{0:T(128)} %constant.45.clone) | copy-start | bytes 232
  0.7 18.2 %copy-start = (f32[19,8,8,128]{3,2,1,0:T(8,128)S(1)}, f32[19,8,8,128]{3,2,1,0:T(8,128)}, u32[]{:S(2)}) copy-start(f32[19,8,8,128]{3,2,1,0:T(8,128)} %param.14) | copy-start | bytes 1867780
  3.2 21.1 %all-to-all-start = ((s32[128,1,8]{2,1,0:T(1,128)}), s32[128,1,8]{2,1,0:T(1,128)S(1)}, u32[]{:S(2)}, u32[]{:S(2)}) async-start(s32[128,1,8]{2,1,0:T(1,128)} %bitcast.8), calls=%async_computation | async-start | bytes 131072 | tf_op jit(solution)/shard_map/all_to_all | solution.py:143
  17.8 2.6 %copy-start.18 = (s32[8,8,128]{2,1,0:T(8,128)S(1)}, s32[8,8,128]{2,1,0:T(8,128)}, u32[]{:S(2)}) copy-start(s32[8,8,128]{2,1,0:T(8,128)} %param.15) | copy-start | bytes 98308
  17.9 3.2 %copy-start.19 = (s32[2,1024]{1,0:T(2,128)S(1)}, s32[2,1024]{1,0:T(2,128)}, u32[]{:S(2)}) copy-start(s32[2,1024]{1,0:T(2,128)} %param.17) | copy-start | bytes 24580
  17.9 6.5 %copy-start.22 = (f32[3,512]{1,0:T(4,128)S(1)}, f32[3,512]{1,0:T(4,128)}, u32[]{:S(2)}) copy-start(f32[3,512]{1,0:T(4,128)} %param.19) | copy-start | bytes 18436
  17.9 6.5 %copy-start.23 = (f32[3,512]{1,0:T(4,128)S(1)}, f32[3,512]{1,0:T(4,128)}, u32[]{:S(2)}) copy-start(f32[3,512]{1,0:T(4,128)} %param.18) | copy-start | bytes 18436
  17.9 6.5 %copy-start.24 = (f32[512]{0:T(512)S(1)}, f32[512]{0:T(512)}, u32[]{:S(2)}) copy-start(f32[512]{0:T(512)} %param.20) | copy-start | bytes 6148
  26.5 20.1 %all-to-all-start.1 = ((f32[7,128,8]{0,2,1:T(8,128)}), f32[7,128,8]{0,2,1:T(8,128)S(1)}, u32[]{:S(2)}, u32[]{:S(2)}) async-start(f32[7,128,8]{0,2,1:T(8,128)} %copy.70), calls=%async_computation.1 | async-start | bytes 1048576 | tf_op jit(solution)/shard_map/all_to_all | solution.py:152
  65.0 7.0 %collective-permute-start = (f32[23,1,8,128]{3,2,1,0:T(8,128)S(1)}, f32[23,1,8,128]{3,2,1,0:T(8,128)S(1)}, u32[]{:S(2)}, u32[]{:S(2)}) collective-permute-start(f32[23,1,8,128]{3,2,1,0:T(8,128)S(1)} %get-tuple-element.137), channel_id=1, source_target_pairs={{0,8},{8,16},{16,24},{24,32},{32,40},{40,48},{48,56},{56,64},{64,7... | collective-permute-start | bytes 282632 | tf_op jit(solution)/shard_map/ppermute | solution.py:44
  65.0 6.9 %collective-permute-start.1 = (f32[23,1,8,128]{3,2,1,0:T(8,128)S(1)}, f32[23,1,8,128]{3,2,1,0:T(8,128)S(1)}, u32[]{:S(2)}, u32[]{:S(2)}) collective-permute-start(f32[23,1,8,128]{3,2,1,0:T(8,128)S(1)} %get-tuple-element.136), channel_id=1, source_target_pairs={{8,0},{16,8},{24,16},{32,24},{40,32},{48,40},{56,48},{64,56},{72,6... | collective-permute-start | bytes 282632 | tf_op jit(solution)/shard_map/ppermute | solution.py:47
  72.1 4.9 %collective-permute-start.2 = (f32[23,10,1,128]{3,2,1,0:T(1,128)S(1)}, f32[23,10,1,128]{3,2,1,0:T(1,128)S(1)}, u32[]{:S(2)}, u32[]{:S(2)}) collective-permute-start(f32[23,10,1,128]{3,2,1,0:T(1,128)S(1)} %get-tuple-element.132), channel_id=1, source_target_pairs={{0,1},{1,2},{2,3},{3,4},{4,5},{5,6},{6,7},{7,0},{8,9},{9,10},{10,1... | collective-permute-start | bytes 353288 | tf_op jit(solution)/shard_map/ppermute | solution.py:44
  74.0 4.5 %collective-permute-start.3 = (f32[23,10,1,128]{3,2,1,0:T(1,128)S(1)}, f32[23,10,1,128]{3,2,1,0:T(1,128)S(1)}, u32[]{:S(2)}, u32[]{:S(2)}) collective-permute-start(f32[23,10,1,128]{3,2,1,0:T(1,128)S(1)} %get-tuple-element.133), channel_id=1, source_target_pairs={{1,0},{2,1},{3,2},{4,3},{5,4},{6,5},{7,6},{0,7},{9,8},{10,9},{11,1... | collective-permute-start | bytes 353288 | tf_op jit(solution)/shard_map/ppermute | solution.py:47
  79.3 0.7 copy-start.16
  80.0 0.8 copy-start.8
  80.1 0.8 copy-start.10
  80.1 0.8 copy-start.12
  80.1 0.8 copy-start.14
  94.3 20.6 %all-to-all-start.2 = ((f32[3,128,8]{2,0,1:T(4,128)}), f32[3,128,8]{2,0,1:T(4,128)S(1)}, u32[]{:S(2)}, u32[]{:S(2)}) async-start(f32[3,128,8]{2,0,1:T(4,128)} %copy.76), calls=%async_computation.2 | async-start | bytes 524288 | tf_op jit(solution)/shard_map/all_to_all | solution.py:180
  103.8 0.9 copy-start.2
  103.8 1.0 copy-start.7
  103.8 1.0 copy-start.13
  103.9 0.9 copy-start.15
  103.9 1.0 copy-start.1
  103.9 1.0 copy-start.9
  103.9 1.0 copy-start.11
  105.1 0.9 copy-start.3
  105.1 1.0 copy-start.4
  105.2 1.0 copy-start.5
  105.2 1.0 copy-start.6
  106.8 0.7 copy-start.17
  107.2 8.6 %copy-start.25 = (f32[512]{0:T(512)S(1)}, f32[512]{0:T(512)}, u32[]{:S(2)}) copy-start(f32[512]{0:T(512)} %param.21) | copy-start | bytes 6148
where the time goes:
time: 118 us; the launch traced here: 117 us
  matrix products  37.1 us (31%)
  starting transfers between devices  34.3 us (29%)
  waiting for transfers between devices  23.8 us (20%)
  local copies, waits for them, and re-layouts  11 us (9%)
  other arithmetic  9.79 us (8%)
    dot_general x8, matrix products, wall_plane(): jnp.einsum('cn,kn->ck', near_wall, indicator(ids, near_count), precision=...  16.1 us
    all_to_all x1, waiting for transfers between devices, local(): lax.all_to_all(answer, ('gx', 'yz'), split_axis=1, concat_axis=1, tiled=T...  12.4 us
    dot_general x8, matrix products, add_plane(): jnp.einsum('ck,kn->cn', forces, indicator(ids, near_count), precision=hig...  11.7 us
    all_to_all x1, starting transfers between devices, local(): lax.all_to_all(near_rows.reshape(devices, slot_count), ('gx', 'yz'), spli...  11.5 us
    all_to_all x1, starting transfers between devices, local(): lax.all_to_all(slot_force.reshape(3, devices, slot_count), ('gx', 'yz'),...  9.48 us
    all_to_all x1, starting transfers between devices, local(): lax.all_to_all(answer, ('gx', 'yz'), split_axis=1, concat_axis=1, tiled=T...  6.56 us
    all_to_all x1, waiting for transfers between devices, local(): lax.all_to_all(slot_force.reshape(3, devices, slot_count), ('gx', 'yz'),...  6.52 us
    ppermute x2, starting transfers between devices, extended(): lax.ppermute(lax.slice_in_dim(block, 0, width, axis=dim), axis, backward)  4.7 us
  transfers between devices with their start and end apart: 7, of which 4 were waited for; matrix products, arithmetic and copies ran while one was open for 13% of the time, Pallas kernels for 0%

commit v1 on v0

v1 whole, which is shorter than its diff:
```python
import jax
import jax.numpy as jnp
from jax import lax
from jax.experimental import pallas as pl
from jax.experimental.pallas import tpu as pltpu
from jax.sharding import PartitionSpec as P

lattice_dirs = (
    (0, 0, 0),
    (1, 0, 0),
    (-1, 0, 0),
    (0, 1, 0),
    (0, -1, 0),
    (0, 0, 1),
    (0, 0, -1),
    (1, 1, 0),
    (-1, -1, 0),
    (1, -1, 0),
    (-1, 1, 0),
    (1, 0, 1),
    (-1, 0, -1),
    (1, 0, -1),
    (-1, 0, 1),
    (0, 1, 1),
    (0, -1, -1),
    (0, 1, -1),
    (0, -1, 1),
)
lattice_weights = (1.0 / 3.0,) + (1.0 / 18.0,) * 6 + (1.0 / 36.0,) * 12
opposite = (0, 2, 1, 4, 3, 6, 5, 8, 7, 10, 9, 12, 11, 14, 13, 16, 15, 18, 17)
relax_rate = 1.25
stiffness = 0.5
damping = 0.5

from_low_x = (1, 7, 9, 11, 13)
from_high_x = (2, 8, 10, 12, 14)
from_low_y = (3, 7, 10, 15, 17)
from_high_y = (4, 8, 9, 16, 18)

fields = ((1, 0, 0), (0, 1, 0), (0, 0, 1), (1, 1, 0), (1, -1, 0), (1, 0, 1), (1, 0, -1), (0, 1, 1), (0, 1, -1))


def field_of(direction):
    vector = lattice_dirs[direction]
    if vector in fields:
        return fields.index(vector), 1.0
    return fields.index(tuple(-c for c in vector)), -1.0


WX, WY, WZ = 8, 8, 128
ROWS = WX * WY
VMEM = pl.BlockSpec(memory_space=pltpu.VMEM)
f32 = jnp.float32
i32 = jnp.int32


def call(kernel, outs, scratch=(), limit=24, flops=1_000_000):
    def run(*args):
        return pl.pallas_call(
            kernel,
            out_shape=[jax.ShapeDtypeStruct(s, d) for s, d in outs],
            in_specs=[VMEM] * len(args),
            out_specs=[VMEM] * len(outs),
            scratch_shapes=list(scratch),
            compiler_params=pltpu.CompilerParams(vmem_limit_bytes=limit << 20),
            cost_estimate=pl.CostEstimate(flops=flops, bytes_accessed=1 << 20, transcendentals=0),
        )(*args)

    return run


def lane_take(table, index):
    return jnp.take_along_axis(table, index, axis=1, mode="promise_in_bounds")


def spread(row):
    return jnp.broadcast_to(row, (8, 128))


def sublane_iota():
    return lax.broadcasted_iota(i32, (8, 128), 0)


def lane_iota():
    return lax.broadcasted_iota(i32, (8, 128), 1)


def collide(pops):
    density = pops[0]
    for direction in range(1, 19):
        density = density + pops[direction]
    inverse = 1.0 / density
    speeds = []
    for compo in range(3):
        moment = None
        for direction in range(1, 19):
            factor = lattice_dirs[direction][compo]
            if factor == 1:
                moment = pops[direction] if moment is None else moment + pops[direction]
            elif factor == -1:
                moment = moment - pops[direction]
        speeds.append(moment * inverse)
    square = speeds[0] * speeds[0] + speeds[1] * speeds[1] + speeds[2] * speeds[2]
    rest = 1.0 - 1.5 * square
    keep = 1.0 - relax_rate
    scaled = relax_rate * density
    post = [None] * 19
    post[0] = keep * pops[0] + (lattice_weights[0] * scaled) * rest
    scale = {w: w * scaled for w in (1.0 / 18.0, 1.0 / 36.0)}
    for direction in range(1, 19, 2):
        along = None
        for compo in range(3):
            factor = lattice_dirs[direction][compo]
            if factor == 1:
                along = speeds[compo] if along is None else along + speeds[compo]
            elif factor == -1:
                along = along - speeds[compo]
        weight = scale[lattice_weights[direction]]
        even = weight * (rest + 4.5 * along * along)
        odd = weight * (3.0 * along)
        post[direction] = keep * pops[direction] + even + odd
        post[direction + 1] = keep * pops[direction + 1] + even - odd
    total = post[0]
    for direction in range(1, 19):
        total = total + post[direction]
    return post, total


def first_kernel(pop, ids, near, g, r, x_up, x_down, y_up, y_down, ask):
    lane = lane_iota()
    sub = sublane_iota()
    for tile in range(16):
        row = near[0:1, (tile // 2) * 128 : (tile // 2) * 128 + 128]
        index = (8 * (tile % 2) + sub) * 8 + (lane & 7)
        ask[tile * 8 : tile * 8 + 8, :] = lane_take(spread(row), index)
    for x in range(WX):
        pops = [pop[c * ROWS + x * 8 : c * ROWS + x * 8 + 8, :] for c in range(19)]
        cell = ids[x * 8 : x * 8 + 8, :]
        fluid = cell < 0
        post, total = collide(pops)
        post = [jnp.where(fluid, p, 0.0) for p in post]
        total = jnp.where(fluid, total, 0.0)
        for c in range(19):
            g[c * ROWS + x * 8 : c * ROWS + x * 8 + 8, :] = post[c]
        r[x * 8 : x * 8 + 8, :] = total
        for at, names, out in ((WX - 1, from_low_x, x_up), (0, from_high_x, x_down)):
            if x == at:
                for k, c in enumerate(names):
                    out[k * 8 : k * 8 + 8, :] = post[c]
                out[40:48, :] = total
                out[48:56, :] = cell.astype(f32)
    for y, names, out in ((WY - 1, from_low_y, y_up), (0, from_high_y, y_down)):
        for k, c in enumerate(names):
            out[k * 8 : k * 8 + 8, :] = g[pl.ds(c * ROWS + y, 8, stride=8), :]
        out[40:48, :] = r[pl.ds(y, 8, stride=8), :]
        out[48:56, :] = ids[pl.ds(y, 8, stride=8), :].astype(f32)


def corner_kernel(y_up, y_down, low, high, out_up, out_down):
    zero = jnp.zeros((2, 128), f32)
    for src, out, y, k_low, k_high in (
        (y_up, out_up, WY - 1, from_low_x.index(7), from_high_x.index(10)),
        (y_down, out_down, 0, from_low_x.index(9), from_high_x.index(8)),
    ):
        out[0:56, :] = src[...]
        for at, halo, k in ((56, low, k_low), (59, high, k_high)):
            out[at : at + 1, :] = halo[k * 8 + y : k * 8 + y + 1, :]
            out[at + 1 : at + 2, :] = halo[40 + y : 41 + y, :]
            out[at + 2 : at + 3, :] = halo[48 + y : 49 + y, :]
        out[62:64, :] = zero


def shift_y(value, c_y, row):
    sub = sublane_iota()
    if c_y == 1:
        return jnp.where(sub == 0, spread(row), pltpu.roll(value, 1, 0))
    return jnp.where(sub == WY - 1, spread(row), pltpu.roll(value, WY - 1, 0))


def shift_z(value, c_z):
    return value if c_z == 0 else pltpu.roll(value, c_z % WZ, 1)


def stencil_kernel(g, r, pop, ids, low, high, y_low, y_high, base, sums, shifted, part, left, hot):
    def y_row(c_y, k, x):
        halo = y_low if c_y == 1 else y_high
        if x == -1:
            at = 56 + (1 if k is None else 0)
        elif x == WX:
            at = 59 + (1 if k is None else 0)
        else:
            at = (5 if k is None else k) * 8 + x
        return halo[at : at + 1, :]

    def source(direction, x):
        c_x, c_y, c_z = lattice_dirs[direction]
        at = x - c_x
        if at == -1:
            k = from_low_x.index(direction)
            value = low[k * 8 : k * 8 + 8, :]
        elif at == WX:
            k = from_high_x.index(direction)
            value = high[k * 8 : k * 8 + 8, :]
        else:
            value = g[direction * ROWS + at * 8 : direction * ROWS + at * 8 + 8, :]
        if c_y != 0:
            k = (from_low_y if c_y == 1 else from_high_y).index(direction)
            value = shift_y(value, c_y, y_row(c_y, k, at))
        return shift_z(value, c_z)

    combos = [(0, 0), (1, 0), (-1, 0), (0, 1), (0, -1), (1, 1), (-1, -1), (1, -1), (-1, 1)]
    for at in range(-1, WX + 1):
        plain = low[40:48, :] if at == -1 else high[40:48, :] if at == WX else r[at * 8 : at * 8 + 8, :]
        by_y = {0: plain}
        for c_y in (1, -1):
            by_y[c_y] = shift_y(plain, c_y, y_row(c_y, None, at))
        for k, (c_y, c_z) in enumerate(combos):
            if c_y != 0 and c_z != 0 and not 0 <= at < WX:
                continue
            shifted[k * 80 + (at + 1) * 8 : k * 80 + (at + 1) * 8 + 8, :] = shift_z(by_y[c_y], c_z)

    sub = sublane_iota()
    total = jnp.zeros((160, 128), f32)
    for x in range(WX):
        rows = slice(x * 8, x * 8 + 8)
        cell = ids[rows, :]
        fluid = cell < 0
        base[x * 8 : x * 8 + 8, :] = jnp.where(fluid, g[x * 8 : x * 8 + 8, :], pop[x * 8 : x * 8 + 8, :])
        acc = [None] * 9

        def add(k, value):
            acc[k] = value if acc[k] is None else acc[k] + value

        for direction in range(1, 19):
            vector = lattice_dirs[direction]
            c_x, c_y, c_z = vector
            k = combos.index((c_y, c_z))
            near_r = shifted[k * 80 + (x - c_x + 1) * 8 : k * 80 + (x - c_x + 1) * 8 + 8, :]
            came = source(direction, x)
            at = direction * ROWS + x * 8
            back = opposite[direction] * ROWS + x * 8
            open_link = jnp.where(near_r != 0.0, came, g[back : back + 8, :])
            base[at : at + 8, :] = jnp.where(fluid, open_link, pop[at : at + 8, :])
            pull = (-6.0 * lattice_weights[direction]) * near_r
            for compo in range(3):
                if vector[compo] == 1:
                    add(compo, came)
                elif vector[compo] == -1:
                    acc[compo] = -came if acc[compo] is None else acc[compo] - came
                if vector[compo] != 0:
                    add(3 + compo, pull)
            for n, (p, q) in enumerate(((0, 1), (0, 2), (1, 2))):
                if vector[p] * vector[q] == 1:
                    add(6 + n, pull)
                elif vector[p] * vector[q] == -1:
                    acc[6 + n] = -pull if acc[6 + n] is None else acc[6 + n] - pull
        for v in range(9):
            value = 2.0 * acc[v] if v < 3 else acc[v]
            head = value.astype(jnp.bfloat16).astype(f32)
            part[v * 8 : v * 8 + 8, :] = head
            part[80 + v * 8 : 80 + v * 8 + 8, :] = value - head
        zero = jnp.zeros((8, 128), f32)
        for y in range(WY):
            key = ids[x * 8 + y : x * 8 + y + 1, :]
            slot = spread(key & 7)
            pick = slot == sub
            for half in range(2):
                rows_v = [
                    jnp.where(pick, spread(part[half * 80 + v * 8 + y : half * 80 + v * 8 + y + 1, :]), 0.0)
                    for v in range(9)
                ] + [zero]
                left[half * 80 : half * 80 + 80, y * 128 : y * 128 + 128] = jnp.concatenate(rows_v, 0).astype(
                    jnp.bfloat16
                )
            owner = jnp.broadcast_to(key >> 3, (128, 128))
            number = lax.broadcasted_iota(i32, (128, 128), 0)
            hot[:, y * 128 : y * 128 + 128] = jnp.where(owner == number, 1.0, 0.0).astype(jnp.bfloat16)
        total = total + lax.dot_general(
            left[...], hot[...], (((1,), (1,)), ((), ())), preferred_element_type=f32
        )
    sums[...] = total[0:72, :] + total[80:152, :]


def reply_kernel(got, pos, vel, rad, sums, out, rows_t):
    rows = got[...].astype(f32).T[0:8, :].astype(i32)
    rows_t[...] = rows
    chunk = rows >> 7
    index = rows & 127
    state = []
    for ref, count in ((pos, 3), (vel, 3), (rad, 1)):
        for c in range(count):
            value = jnp.zeros((8, 128), f32)
            for k in range(4):
                table = spread(ref[c : c + 1, k * 128 : k * 128 + 128])
                value = jnp.where(chunk == k, lane_take(table, index), value)
            state.append(value)
    out[pl.ds(0, 128, stride=2), :] = jnp.concatenate(state + [sums[...]], 0).T
    lane = lane_iota()
    side = {-1: (lane & -8) | ((lane - 1) & 7), 1: (lane & -8) | ((lane + 1) & 7)}

    def moved(value, d_x, d_y):
        if d_x != 0:
            value = pltpu.roll(value, 8 if d_x == -1 else 120, 1)
        return value if d_y == 0 else lane_take(value, side[d_y])

    speed = state[3:6]
    plus = speed[0] + speed[1]
    minus = speed[0] - speed[1]
    rest = []
    for d_x, d_y in ((-1, 0), (1, 0), (0, -1), (0, 1)):
        rest += [moved(value, d_x, d_y) for value in speed]
    for d_x, d_y, value in ((-1, -1, plus), (-1, 1, minus), (1, -1, minus), (1, 1, plus)):
        rest.append(moved(value, d_x, d_y))
    out[pl.ds(1, 128, stride=2), :] = jnp.concatenate(rest, 0).T


def last_kernel(
    got, rows_t, base, r, ids, low, high, y_low, y_high, pairs, pos, vel, rad, mass,
    read, vel_next, pos_next,
    table, around, moving, rim, left, hot, pair,
):
    table[...] = got[pl.ds(0, 128, stride=2), :].T
    around[...] = got[pl.ds(1, 128, stride=2), :].T

    def look_up(ref, starts, cell):
        owner = (cell >> 3) & 127
        slot = jnp.where(cell >= 0, cell & 7, 8)
        values = [jnp.zeros((8, 128), f32) for start in starts]
        for s in range(8):
            chosen = slot == s
            for n, start in enumerate(starts):
                taken = lane_take(spread(ref[start + s : start + s + 1, :]), owner)
                values[n] = jnp.where(chosen, taken, values[n])
        return values

    def combine(values, vector):
        total = None
        for value, factor in zip(values, vector):
            if factor == 1:
                total = value if total is None else total + value
            elif factor == -1:
                total = total - value
        return total

    for x in range(WX):
        speeds = look_up(table, (24, 32, 40), ids[x * 8 : x * 8 + 8, :])
        for n, vector in enumerate(fields):
            moving[n * 80 + (x + 1) * 8 : n * 80 + (x + 1) * 8 + 8, :] = combine(speeds, vector)
    for at, halo, start in ((-1, low, 0), (WX, high, 24)):
        speeds = look_up(around, (start, start + 8, start + 16), halo[48:56, :].astype(i32))
        for n, vector in enumerate(fields):
            if vector[0] != 0:
                moving[n * 80 + (at + 1) * 8 : n * 80 + (at + 1) * 8 + 8, :] = combine(speeds, vector)
    for side, halo, start, first, second in ((0, y_low, 48, 96, 112), (1, y_high, 72, 104, 120)):
        speeds = look_up(around, (start, start + 8, start + 16), halo[48:56, :].astype(i32))
        for n, vector in enumerate(fields):
            if vector[1] != 0:
                rim[side * 88 + n * 8 : side * 88 + n * 8 + 8, :] = combine(speeds, vector)
        for n, (row, start_row) in enumerate(((58, first), (61, second))):
            (value,) = look_up(around, (start_row,), spread(halo[row : row + 1, :]).astype(i32))
            rim[side * 88 + 72 + n * 8 : side * 88 + 80 + n * 8, :] = value

    for x in range(WX):
        mine = r[x * 8 : x * 8 + 8, :]
        read[x * 8 : x * 8 + 8, :] = base[x * 8 : x * 8 + 8, :]
        for direction in range(1, 19):
            c_x, c_y, c_z = lattice_dirs[direction]
            n, sign = field_of(direction)
            at = x - c_x
            value = moving[n * 80 + (at + 1) * 8 : n * 80 + (at + 1) * 8 + 8, :]
            if c_y != 0:
                side = 0 if c_y == 1 else 1
                row = side * 88 + (72 if at == -1 else 80 if at == WX else n * 8 + at)
                value = shift_y(value, c_y, rim[row : row + 1, :])
            value = shift_z(value, c_z)
            to = direction * ROWS + x * 8
            read[to : to + 8, :] = base[to : to + 8, :] + ((sign * 6.0 * lattice_weights[direction]) * mine) * value

    for k in range(8):
        pair[k : k + 1, :] = pairs[0:1, k * 128 : k * 128 + 128]
        pair[8 + k : 9 + k, :] = pairs[1:2, k * 128 : k * 128 + 128]
    first = pair[0:8, :]
    second = pair[8:16, :]
    chunk = first >> 7
    index = first & 127
    state_a = []
    for ref, count in ((pos, 3), (vel, 3), (rad, 1)):
        for c in range(count):
            value = jnp.zeros((8, 128), f32)
            for k in range(4):
                value = jnp.where(
                    chunk == k, lane_take(spread(ref[c : c + 1, k * 128 : k * 128 + 128]), index), value
                )
            state_a.append(value)
    state_b = look_up(table, tuple(8 * c for c in range(7)), second)
    offset = [a - b for a, b in zip(state_a[0:3], state_b[0:3])]
    length = jnp.sqrt(offset[0] * offset[0] + offset[1] * offset[1] + offset[2] * offset[2])
    inverse = 1.0 / jnp.maximum(length, 1.0)
    normal = [o * inverse for o in offset]
    inter = jnp.maximum(state_a[6] + state_b[6] - length, 0.0)
    closing = None
    for a, b, n in zip(state_a[3:6], state_b[3:6], normal):
        closing = (a - b) * n if closing is None else closing + (a - b) * n
    size = stiffness * inter - damping * inter * closing
    push = [size * n for n in normal]

    left[...] = jnp.zeros((16, 2048), f32)
    number = lax.broadcasted_iota(i32, (512, 128), 0)
    for s in range(8):
        left[0:9, s * 128 : s * 128 + 128] = table[pl.ds(56 + s, 9, stride=8), :]
        key = jnp.broadcast_to(rows_t[s : s + 1, :], (512, 128))
        hot[:, s * 128 : s * 128 + 128] = jnp.where(key == number, 1.0, 0.0).astype(jnp.bfloat16)
    for k in range(8):
        columns = slice(1024 + k * 128, 1024 + k * 128 + 128)
        for c in range(3):
            left[9 + c : 10 + c, columns] = push[c][k : k + 1, :]
        key = jnp.broadcast_to(pairs[0:1, k * 128 : k * 128 + 128], (512, 128))
        hot[:, columns] = jnp.where(key == number, 1.0, 0.0).astype(jnp.bfloat16)
    values = left[...]
    head = values.astype(jnp.bfloat16)
    tail = (values - head.astype(f32)).astype(jnp.bfloat16)
    by_grain = lax.dot_general(
        jnp.concatenate([head, tail], 0), hot[...], (((1,), (1,)), ((), ())), preferred_element_type=f32
    )
    by_grain = by_grain[0:16, :] + by_grain[16:32, :]
    part = [by_grain[n : n + 1, :] for n in range(12)]
    speed = [vel[c : c + 1, :] for c in range(3)]
    matrix = ((3, 6, 7), (6, 4, 8), (7, 8, 5))
    for c in range(3):
        force = part[c]
        for q in range(3):
            force = force + part[matrix[c][q]] * speed[q]
        fresh = speed[c] + (force + part[9 + c]) / mass[...]
        vel_next[c : c + 1, :] = fresh
        pos_next[c : c + 1, :] = pos[c : c + 1, :] + fresh


def ring(axis, value, up):
    count = lax.axis_size(axis)
    pairs = [(i, (i + 1) % count) if up else ((i + 1) % count, i) for i in range(count)]
    return lax.ppermute(value, axis, pairs)


def exchange(value):
    return lax.all_to_all(value, ("gx", "yz"), split_axis=0, concat_axis=0, tiled=True)


def local(
    populations,
    cell_grain,
    near_rows,
    contact_pairs,
    grain_position,
    grain_velocity,
    grain_radius,
    grain_mass,
):
    pop = populations.reshape(19 * ROWS, 128)
    ids = cell_grain.reshape(ROWS, 128)
    rad = grain_radius.reshape(1, 512)
    mass = grain_mass.reshape(1, 512)
    slab = (56, 128)
    full = (19 * ROWS, 128)
    g, r, x_up, x_down, y_up, y_down, ask = call(
        first_kernel,
        [(full, f32), ((ROWS, 128), f32), (slab, f32), (slab, f32), (slab, f32), (slab, f32), ((128, 128), i32)],
    )(pop, ids, near_rows)
    low = ring("gx", x_up, True)
    high = ring("gx", x_down, False)
    asked = exchange(ask)
    y_up, y_down = call(corner_kernel, [((64, 128), f32), ((64, 128), f32)])(y_up, y_down, low, high)
    y_low = ring("yz", y_up, True)
    y_high = ring("yz", y_down, False)
    base, sums = call(
        stencil_kernel,
        [(full, f32), ((72, 128), f32)],
        [
            pltpu.VMEM((9 * 80, 128), f32),
            pltpu.VMEM((160, 128), f32),
            pltpu.VMEM((160, 1024), jnp.bfloat16),
            pltpu.VMEM((128, 1024), jnp.bfloat16),
        ],
    )(g, r, pop, ids, low, high, y_low, y_high)
    send, rows_t = call(reply_kernel, [((256, 128), f32), ((8, 128), i32)])(
        asked, grain_position, grain_velocity, rad, sums
    )
    got = exchange(send.reshape(128, 2, 128)).reshape(256, 128)
    read, vel_next, pos_next = call(
        last_kernel,
        [(full, f32), ((3, 512), f32), ((3, 512), f32)],
        [
            pltpu.VMEM((128, 128), f32),
            pltpu.VMEM((128, 128), f32),
            pltpu.VMEM((9 * 80, 128), f32),
            pltpu.VMEM((2 * 88, 128), f32),
            pltpu.VMEM((16, 2048), f32),
            pltpu.VMEM((512, 2048), jnp.bfloat16),
            pltpu.VMEM((16, 128), i32),
        ],
    )(got, rows_t, base, r, ids, low, high, y_low, y_high, contact_pairs, grain_position, grain_velocity, rad, mass)
    return (read.reshape(19, WX, WY, WZ), vel_next, pos_next)


def solution(mesh):
    return jax.shard_map(
        local,
        mesh=mesh,
        in_specs=(
            P(None, "gx", "yz", None),
            P("gx", "yz", None),
            P(("gx", "yz"), None),
            P(None, ("gx", "yz")),
            P(None, ("gx", "yz")),
            P(None, ("gx", "yz")),
            P(("gx", "yz")),
            P(("gx", "yz")),
        ),
        out_specs=(P(None, "gx", "yz", None), P(None, ("gx", "yz")), P(None, ("gx", "yz"))),
        check_vma=False,
    )
```

time: 118 us -> 53.2 us (0.45)
  matrix products: 37.1 us -> 0 us
  blocking collectives: 0 us -> 18.9 us
  waiting for transfers between devices: 23.8 us -> 5.15 us
  starting transfers between devices: 34.3 us -> 18.9 us
  other arithmetic: 9.79 us -> 0 us
  local copies, waits for them, and re-layouts: 11 us -> 3.87 us
  Pallas kernels: 0 us -> 5.35 us
    dot_general x23 -> x0, matrix products: 37.1 us -> none  [the longest x8 16.1 us: wall_plane(): jnp.einsum('cn,kn->ck', near_wall, indicator(ids, near_count), precision=...]
    all_to_all x3 -> x1, waiting for transfers between devices: 22.2 us -> 0.01 us  [exchange(): lax.all_to_all(value, ('gx', 'yz'), split_axis=0, concat_axis=0, tiled=True)]
    all_to_all x0 -> x1, blocking collectives: none -> 18.9 us  [exchange(): lax.all_to_all(value, ('gx', 'yz'), split_axis=0, concat_axis=0, tiled=True)]
    all_to_all x3 -> x1, starting transfers between devices: 27.5 us -> 11.5 us  [exchange(): lax.all_to_all(value, ('gx', 'yz'), split_axis=0, concat_axis=0, tiled=True)]
    pallas_call x0 -> x5, Pallas kernels: none -> 5.35 us  [run(): pl.pallas_call(kernel, out_shape=[jax.ShapeDtypeStruct(s, d) for s, d in...]
    slice x12 -> x0, local copies, waits for them, and re-layouts: 4.98 us -> none  [the longest x8 4.52 us: shifted(): piece = jnp.roll(piece, shift_z, axis=3)]
    ppermute x4, waiting for transfers between devices: 1.59 us -> 5.15 us  [ring(): return lax.ppermute(value, axis, pairs)]
    unnamed x19 -> x0, other arithmetic: 2.96 us -> none
  transfers between devices with their start and end apart: 7 -> 5, of which waited for: 4 -> 3; matrix products, arithmetic and copies ran while one was open for 13% -> 0% of each run, Pallas kernels for 0% -> 4%
where the time goes in v1:
time: 53.2 us; the launch traced here: 52.9 us
  starting transfers between devices  18.9 us (36%)
  blocking collectives  18.9 us (36%)
  Pallas kernels  5.35 us (10%)
  waiting for transfers between devices  5.15 us (10%)
  local copies, waits for them, and re-layouts  3.87 us (7%)
  between operations  0.72 us (1%)
    all_to_all x1, blocking collectives, exchange(): lax.all_to_all(value, ('gx', 'yz'), split_axis=0, concat_axis=0, tiled=True)  18.9 us
    all_to_all x1, starting transfers between devices, exchange(): lax.all_to_all(value, ('gx', 'yz'), split_axis=0, concat_axis=0, tiled=True)  11.5 us
    ppermute x4, starting transfers between devices, ring(): return lax.ppermute(value, axis, pairs)  7.45 us
    pallas_call x5, Pallas kernels, run(): pl.pallas_call(kernel, out_shape=[jax.ShapeDtypeStruct(s, d) for s, d in...  5.35 us
    ppermute x4, waiting for transfers between devices, ring(): return lax.ppermute(value, axis, pairs)  5.15 us
    unnamed x20, local copies, waits for them, and re-layouts  3.87 us
  transfers between devices with their start and end apart: 5, of which 3 were waited for; matrix products, arithmetic and copies ran while one was open for 0% of the time, Pallas kernels for 4%

profile of v1, /device:TPU:1, one launch (start us, length us, event | category | flops | bytes accessed | tf_op | source)
XLA Modules:
  0.0 52.9 jit_solution(12980529910761835829)
XLA Ops:
  0.6 0.0 copy-start
  0.6 1.1 %copy-done = f32[19,8,8,128]{3,2,1,0:T(8,128)S(1)} copy-done((f32[19,8,8,128]{3,2,1,0:T(8,128)S(1)}, f32[19,8,8,128]{3,2,1,0:T(8,128)}, u32[]{:S(2)}) %copy-start) | copy-done | bytes 622616
  1.7 0.0 copy-start.2
  1.7 0.8 %copy-done.2 = s32[8,8,128]{2,1,0:T(8,128)S(1)} copy-done((s32[8,8,128]{2,1,0:T(8,128)S(1)}, s32[8,8,128]{2,1,0:T(8,128)}, u32[]{:S(2)}) %copy-start.2) | copy-done | bytes 32792
  2.5 0.0 copy-start.8
  2.5 0.7 %copy-done.8 = s32[1,1024]{1,0:T(1,128)S(1)} copy-done((s32[1,1024]{1,0:T(1,128)S(1)}, s32[1,1024]{1,0:T(1,128)}, u32[]{:S(2)}) %copy-start.8) | copy-done | bytes 4120
  3.2 0.0 copy-start.1
  3.2 0.7 %shard_map.103 = (f32[1216,128]{1,0:T(8,128)S(1)}, f32[64,128]{1,0:T(8,128)S(1)}, f32[56,128]{1,0:T(8,128)S(1)}, f32[56,128]{1,0:T(8,128)S(1)}, f32[56,128]{1,0:...) custom-call(f32[1216,128]{1,0:T(8,128)S(1)} %bitcast.11, s32[64,128]{1,0:T(8,128)S(1)} %bitcast.14, ...), custom_call_target="tpu_custom_call" | custom-call | flops 1000000 | bytes 1048576 | tf_op jit(solution)/shard_map/pallas_call | solution.py:59
  3.9 11.5 %all-to-all-start = ((s32[128,1,128]{2,1,0:T(1,128)}), s32[128,1,128]{2,1,0:T(1,128)S(1)}, u32[]{:S(2)}, u32[]{:S(2)}) async-start(s32[128,1,128]{2,1,0:T(1,128)} %bitcast.3), calls=%async_computation | async-start | bytes 131072 | tf_op jit(solution)/shard_map/all_to_all | solution.py:445
  15.4 1.4 %collective-permute-start = (f32[56,128]{1,0:T(8,128)S(1)}, f32[56,128]{1,0:T(8,128)S(1)}, u32[]{:S(2)}, u32[]{:S(2)}) collective-permute-start(f32[56,128]{1,0:T(8,128)S(1)} %get-tuple-element.22), channel_id=1, source_target_pairs={{0,8},{8,16},{16,24},{24,32},{32,40},{40,48},{48,56},{56,64},{64,7... | collective-permute-start | bytes 86024 | tf_op jit(solution)/shard_map/ppermute | solution.py:441
  16.8 4.1 %collective-permute-start.1 = (f32[56,128]{1,0:T(8,128)S(1)}, f32[56,128]{1,0:T(8,128)S(1)}, u32[]{:S(2)}, u32[]{:S(2)}) collective-permute-start(f32[56,128]{1,0:T(8,128)S(1)} %get-tuple-element.23), channel_id=1, source_target_pairs={{8,0},{16,8},{24,16},{32,24},{40,32},{48,40},{56,48},{64,56},{72,6... | collective-permute-start | bytes 86024 | tf_op jit(solution)/shard_map/ppermute | solution.py:441
  20.9 1.8 %collective-permute-done.low = f32[56,128]{1,0:T(8,128)S(1)} collective-permute-done((f32[56,128]{1,0:T(8,128)S(1)}, f32[56,128]{1,0:T(8,128)S(1)}, u32[]{:S(2)}, u32[]{:S(2)}) %collective-permute-start) | collective-permute-done | bytes 28704 | tf_op jit(solution)/shard_map/ppermute | solution.py:441
  22.7 0.0 collective-permute-done.1.high
  22.7 0.0 copy-start.3
  22.8 1.9 %collective-permute-start.2 = (f32[64,128]{1,0:T(8,128)S(1)}, f32[64,128]{1,0:T(8,128)S(1)}, u32[]{:S(2)}, u32[]{:S(2)}) collective-permute-start(f32[64,128]{1,0:T(8,128)S(1)} %get-tuple-element.26), channel_id=1, source_target_pairs={{0,1},{1,2},{2,3},{3,4},{4,5},{5,6},{6,7},{7,0},{8,9},{9,10},{10,1... | collective-permute-start | bytes 98312 | tf_op jit(solution)/shard_map/ppermute | solution.py:441
  24.7 0.0 collective-permute-start.3
  24.7 1.0 %collective-permute-done.2.y_low = f32[64,128]{1,0:T(8,128)S(1)} collective-permute-done((f32[64,128]{1,0:T(8,128)S(1)}, f32[64,128]{1,0:T(8,128)S(1)}, u32[]{:S(2)}, u32[]{:S(2)}) %collective-permute-start.2) | collective-permute-done | bytes 32800 | tf_op jit(solution)/shard_map/ppermute | solution.py:441
  25.7 2.3 %collective-permute-done.3.y_high = f32[64,128]{1,0:T(8,128)S(1)} collective-permute-done((f32[64,128]{1,0:T(8,128)S(1)}, f32[64,128]{1,0:T(8,128)S(1)}, u32[]{:S(2)}, u32[]{:S(2)}) %collective-permute-start.3) | collective-permute-done | bytes 32800 | tf_op jit(solution)/shard_map/ppermute | solution.py:441
  28.0 0.0 copy-done.1
  28.0 0.0 copy-done.3
  28.0 0.0 copy-start.4
  28.0 0.0 copy-start.5
  28.0 2.3 %shard_map.105 = (f32[1216,128]{1,0:T(8,128)S(1)}, f32[72,128]{1,0:T(8,128)S(1)}) custom-call(f32[1216,128]{1,0:T(8,128)S(1)} %get-tuple-element.20.g, f32[64,128]{1,0:T(8,128)S(1)} %get-tuple-element.21.r, f32[1216,128]{1,0:T(8,128)S(1)} %bitcast.12, s32[64,128]{1,0:T(8,128)S(1)} %bitcast.15, f32[56,128]{1,0:T(8,128)S(1)} %collective-permute-done.low, ...), custom_call_target="tpu_custom_call" | custom-call | flops 1000000 | bytes 1048576 | tf_op jit(solution)/shard_map/pallas_call | solution.py:59
  30.3 0.0 all-to-all-done
  30.3 0.0 copy-start.7
  30.3 0.0 copy-done.4
  30.3 0.0 copy-done.5
  30.3 0.7 %copy-done.7 = f32[512]{0:T(512)S(1)} copy-done((f32[512]{0:T(512)S(1)}, f32[512]{0:T(512)}, u32[]{:S(2)}) %copy-start.7) | copy-done | bytes 2072
  31.0 0.4 shard_map.106
  31.3 0.0 copy-start.6
  31.4 18.9 %all_to_all.16 = f32[128,2,128]{2,1,0:T(2,128)S(1)} all-to-all(f32[128,2,128]{2,1,0:T(2,128)S(1)} %bitcast.18), channel_id=1, replica_groups=mesh['gx'=16,'yz'=8] {'gx','yz'}, dimensions={0} | all-to-all | bytes 262144 | tf_op jit(solution)/shard_map/all_to_all | solution.py:445
  50.2 0.0 copy-start.9
  50.2 0.0 copy-done.6
  50.2 0.7 %copy-done.9 = f32[512]{0:T(512)S(1)} copy-done((f32[512]{0:T(512)S(1)}, f32[512]{0:T(512)}, u32[]{:S(2)}) %copy-start.9) | copy-done | bytes 2072
  50.9 2.0 %shard_map.107 = (f32[1216,128]{1,0:T(8,128)}, f32[3,512]{1,0:T(4,128)}, f32[3,512]{1,0:T(4,128)}) custom-call(f32[256,128]{1,0:T(8,128)S(1)} %bitcast.13, s32[8,128]{1,0:T(8,128)S(1)} %get-tuple-element.30.rows_t, f32[1216,128]{1,0:T(8,128)S(1)} %get-tuple-element.31.base, f32[64,128]{1,0:T(8,128)S(1)} %get-tuple-element.21.r, s32[64,128]{1,0:T(8,128)S(1)} %bitcast.16, ...), custom_call_target="tpu_custom_call" | custom-call | flops 1000000 | bytes 1048576 | tf_op jit(solution)/shard_map/pallas_call | solution.py:59
  (1 shorter events, 0.0 us)
Async XLA Ops:
  0.6 1.1 %copy-start = (f32[19,8,8,128]{3,2,1,0:T(8,128)S(1)}, f32[19,8,8,128]{3,2,1,0:T(8,128)}, u32[]{:S(2)}) copy-start(f32[19,8,8,128]{3,2,1,0:T(8,128)} %param.8) | copy-start | bytes 1867780
  1.7 0.8 %copy-start.2 = (s32[8,8,128]{2,1,0:T(8,128)S(1)}, s32[8,8,128]{2,1,0:T(8,128)}, u32[]{:S(2)}) copy-start(s32[8,8,128]{2,1,0:T(8,128)} %param.9) | copy-start | bytes 98308
  2.5 0.7 %copy-start.8 = (s32[1,1024]{1,0:T(1,128)S(1)}, s32[1,1024]{1,0:T(1,128)}, u32[]{:S(2)}) copy-start(s32[1,1024]{1,0:T(1,128)} %near.1) | copy-start | bytes 12292
  3.2 24.9 %copy-start.1 = (f32[19,8,8,128]{3,2,1,0:T(8,128)S(1)}, f32[19,8,8,128]{3,2,1,0:T(8,128)}, u32[]{:S(2)}) copy-start(f32[19,8,8,128]{3,2,1,0:T(8,128)} %param.8) | copy-start | bytes 1867780
  3.9 26.4 %all-to-all-start = ((s32[128,1,128]{2,1,0:T(1,128)}), s32[128,1,128]{2,1,0:T(1,128)S(1)}, u32[]{:S(2)}, u32[]{:S(2)}) async-start(s32[128,1,128]{2,1,0:T(1,128)} %bitcast.3), calls=%async_computation | async-start | bytes 131072 | tf_op jit(solution)/shard_map/all_to_all | solution.py:445
  15.4 7.3 %collective-permute-start = (f32[56,128]{1,0:T(8,128)S(1)}, f32[56,128]{1,0:T(8,128)S(1)}, u32[]{:S(2)}, u32[]{:S(2)}) collective-permute-start(f32[56,128]{1,0:T(8,128)S(1)} %get-tuple-element.22), channel_id=1, source_target_pairs={{0,8},{8,16},{16,24},{24,32},{32,40},{40,48},{48,56},{56,64},{64,7... | collective-permute-start | bytes 86024 | tf_op jit(solution)/shard_map/ppermute | solution.py:441
  16.8 5.9 %collective-permute-start.1 = (f32[56,128]{1,0:T(8,128)S(1)}, f32[56,128]{1,0:T(8,128)S(1)}, u32[]{:S(2)}, u32[]{:S(2)}) collective-permute-start(f32[56,128]{1,0:T(8,128)S(1)} %get-tuple-element.23), channel_id=1, source_target_pairs={{8,0},{16,8},{24,16},{32,24},{40,32},{48,40},{56,48},{64,56},{72,6... | collective-permute-start | bytes 86024 | tf_op jit(solution)/shard_map/ppermute | solution.py:441
  22.7 5.3 %copy-start.3 = (s32[8,8,128]{2,1,0:T(8,128)S(1)}, s32[8,8,128]{2,1,0:T(8,128)}, u32[]{:S(2)}) copy-start(s32[8,8,128]{2,1,0:T(8,128)} %param.9) | copy-start | bytes 98308
  22.8 2.9 %collective-permute-start.2 = (f32[64,128]{1,0:T(8,128)S(1)}, f32[64,128]{1,0:T(8,128)S(1)}, u32[]{:S(2)}, u32[]{:S(2)}) collective-permute-start(f32[64,128]{1,0:T(8,128)S(1)} %get-tuple-element.26), channel_id=1, source_target_pairs={{0,1},{1,2},{2,3},{3,4},{4,5},{5,6},{6,7},{7,0},{8,9},{9,10},{10,1... | collective-permute-start | bytes 98312 | tf_op jit(solution)/shard_map/ppermute | solution.py:441
  24.7 3.3 %collective-permute-start.3 = (f32[64,128]{1,0:T(8,128)S(1)}, f32[64,128]{1,0:T(8,128)S(1)}, u32[]{:S(2)}, u32[]{:S(2)}) collective-permute-start(f32[64,128]{1,0:T(8,128)S(1)} %get-tuple-element.27), channel_id=1, source_target_pairs={{1,0},{2,1},{3,2},{4,3},{5,4},{6,5},{7,6},{0,7},{9,8},{10,9},{11,1... | collective-permute-start | bytes 98312 | tf_op jit(solution)/shard_map/ppermute | solution.py:441
  28.0 2.3 %copy-start.4 = (f32[3,512]{1,0:T(4,128)S(1)}, f32[3,512]{1,0:T(4,128)}, u32[]{:S(2)}) copy-start(f32[3,512]{1,0:T(4,128)} %pos.3) | copy-start | bytes 18436
  28.0 2.3 %copy-start.5 = (f32[3,512]{1,0:T(4,128)S(1)}, f32[3,512]{1,0:T(4,128)}, u32[]{:S(2)}) copy-start(f32[3,512]{1,0:T(4,128)} %vel.3) | copy-start | bytes 18436
  30.3 0.7 %copy-start.7 = (f32[512]{0:T(512)S(1)}, f32[512]{0:T(512)}, u32[]{:S(2)}) copy-start(f32[512]{0:T(512)} %param.14) | copy-start | bytes 6148
  31.3 18.9 %copy-start.6 = (s32[2,1024]{1,0:T(2,128)S(1)}, s32[2,1024]{1,0:T(2,128)}, u32[]{:S(2)}) copy-start(s32[2,1024]{1,0:T(2,128)} %pairs.1) | copy-start | bytes 24580
  50.2 0.7 %copy-start.9 = (f32[512]{0:T(512)S(1)}, f32[512]{0:T(512)}, u32[]{:S(2)}) copy-start(f32[512]{0:T(512)} %param.15) | copy-start | bytes 6148

commit v2 on v1

--- a/solution.py
+++ b/solution.py
@@ -4,6 +4,7 @@
 from jax.experimental import pallas as pl
 from jax.experimental.pallas import tpu as pltpu
 from jax.sharding import PartitionSpec as P
+
 
 lattice_dirs = (
     (0, 0, 0),
@@ -50,18 +51,20 @@
 WX, WY, WZ = 8, 8, 128
 ROWS = WX * WY
 VMEM = pl.BlockSpec(memory_space=pltpu.VMEM)
+HBM = pl.BlockSpec(memory_space=pltpu.HBM)
 f32 = jnp.float32
 i32 = jnp.int32
 
 
-def call(kernel, outs, scratch=(), limit=24, flops=1_000_000):
+def call(kernel, outs, scratch=(), limit=24, flops=1_000_000, in_specs=None, out_specs=None, aliases=None):
     def run(*args):
         return pl.pallas_call(
             kernel,
             out_shape=[jax.ShapeDtypeStruct(s, d) for s, d in outs],
-            in_specs=[VMEM] * len(args),
-            out_specs=[VMEM] * len(outs),
+            in_specs=in_specs or [VMEM] * len(args),
+            out_specs=out_specs or [VMEM] * len(outs),
             scratch_shapes=list(scratch),
+            input_output_aliases=aliases or {},
             compiler_params=pltpu.CompilerParams(vmem_limit_bytes=limit << 20),
             cost_estimate=pl.CostEstimate(flops=flops, bytes_accessed=1 << 20, transcendentals=0),
         )(*args)
@@ -126,13 +129,39 @@
     return post, total
 
 
-def first_kernel(pop, ids, near, g, r, x_up, x_down, y_up, y_down, ask):
+def first_kernel(
+    pop_in, ids_in, near_in, pairs_in, pos_in, vel_in, rad_in, mass_in,
+    pop, ids, pairs, pos, vel, rad, mass, g, r, x_up, x_down, y_up, y_down, ask_out,
+    near, ask, sems,
+):
+    copies = [
+        pltpu.make_async_copy(src, dst, sems.at[k])
+        for k, (src, dst) in enumerate(
+            (
+                (near_in, near),
+                (ids_in, ids),
+                (pop_in, pop),
+                (pairs_in, pairs),
+                (pos_in, pos),
+                (vel_in, vel),
+                (rad_in, rad),
+                (mass_in, mass),
+            )
+        )
+    ]
+    for copy in copies:
+        copy.start()
+    copies[0].wait()
     lane = lane_iota()
     sub = sublane_iota()
     for tile in range(16):
         row = near[0:1, (tile // 2) * 128 : (tile // 2) * 128 + 128]
         index = (8 * (tile % 2) + sub) * 8 + (lane & 7)
         ask[tile * 8 : tile * 8 + 8, :] = lane_take(spread(row), index)
+    sent = pltpu.make_async_copy(ask, ask_out, sems.at[8])
+    sent.start()
+    copies[1].wait()
+    copies[2].wait()
     for x in range(WX):
         pops = [pop[c * ROWS + x * 8 : c * ROWS + x * 8 + 8, :] for c in range(19)]
         cell = ids[x * 8 : x * 8 + 8, :]
@@ -154,6 +183,9 @@
             out[k * 8 : k * 8 + 8, :] = g[pl.ds(c * ROWS + y, 8, stride=8), :]
         out[40:48, :] = r[pl.ds(y, 8, stride=8), :]
         out[48:56, :] = ids[pl.ds(y, 8, stride=8), :].astype(f32)
+    for copy in copies[3:]:
+        copy.wait()
+    sent.wait()
 
 
 def corner_kernel(y_up, y_down, low, high, out_up, out_down):
@@ -181,7 +213,101 @@
     return value if c_z == 0 else pltpu.roll(value, c_z % WZ, 1)
 
 
-def stencil_kernel(g, r, pop, ids, low, high, y_low, y_high, base, sums, shifted, part, left, hot):
+combos = ((0, 0), (1, 0), (-1, 0), (0, 1), (0, -1), (1, 1), (-1, -1), (1, -1), (-1, 1))
+
+
+class Totals:
+    def __init__(self, start=None):
+        self.acc = start or [None] * 9
+
+    def add(self, k, value, sign):
+        if self.acc[k] is None:
+            self.acc[k] = value if sign == 1 else -value
+        else:
+            self.acc[k] = self.acc[k] + value if sign == 1 else self.acc[k] - value
+
+    def link(self, direction, came, near_r):
+        vector = lattice_dirs[direction]
+        pull = (-6.0 * lattice_weights[direction]) * near_r
+        for compo in range(3):
+            if vector[compo] != 0:
+                self.add(compo, came, vector[compo])
+                self.add(3 + compo, pull, 1)
+        for n, (p, q) in enumerate(((0, 1), (0, 2), (1, 2))):
+            if vector[p] * vector[q] != 0:
+                self.add(6 + n, pull, vector[p] * vector[q])
+
+
+def stream(base, g, pop, fluid, direction, x, came, near_r):
+    at = direction * ROWS + x * 8
+    back = opposite[direction] * ROWS + x * 8
+    open_link = jnp.where(near_r != 0.0, came, g[back : back + 8, :])
+    base[at : at + 8, :] = jnp.where(fluid, open_link, pop[at : at + 8, :])
+
+
+def source_plane(g, low, high, direction, at):
+    if at == -1:
+        k = from_low_x.index(direction)
+        return low[k * 8 : k * 8 + 8, :]
+    if at == WX:
+        k = from_high_x.index(direction)
+        return high[k * 8 : k * 8 + 8, :]
+    return g[direction * ROWS + at * 8 : direction * ROWS + at * 8 + 8, :]
+
+
+def density_plane(r, low, high, at):
+    return low[40:48, :] if at == -1 else high[40:48, :] if at == WX else r[at * 8 : at * 8 + 8, :]
+
+
+def early_kernel(g, r, pop, ids, low, high, pairs, pos, vel, rad, base, forces, hot, pair_hot, state, shifted, pair):
+    for at in range(-1, WX + 1):
+        plain = density_plane(r, low, high, at)
+        for k, c_z in enumerate((0, 1, -1)):
+            shifted[k * 80 + (at + 1) * 8 : k * 80 + (at + 1) * 8 + 8, :] = shift_z(plain, c_z)
+    for x in range(WX):
+        fluid = ids[x * 8 : x * 8 + 8, :] < 0
+        base[x * 8 : x * 8 + 8, :] = jnp.where(fluid, g[x * 8 : x * 8 + 8, :], pop[x * 8 : x * 8 + 8, :])
+        sums = Totals()
+        for direction in range(1, 19):
+            c_x, c_y, c_z = lattice_dirs[direction]
+            if c_y != 0:
+                continue
+            at = x - c_x
+            row = (0, 1, -1).index(c_z) * 80 + (at + 1) * 8
+            near_r = shifted[row : row + 8, :]
+            came = shift_z(source_plane(g, low, high, direction, at), c_z)
+            stream(base, g, pop, fluid, direction, x, came, near_r)
+            sums.link(direction, came, near_r)
+        for v in (0, 2, 3, 5, 7):
+            forces[v * ROWS + x * 8 : v * ROWS + x * 8 + 8, :] = sums.acc[v]
+    number = lax.broadcasted_iota(i32, (128, 128), 0)
+    for row in range(ROWS):
+        owner = jnp.broadcast_to(ids[row : row + 1, :] >> 3, (128, 128))
+        hot[:, row * 128 : row * 128 + 128] = jnp.where(owner == number, 1.0, 0.0).astype(jnp.bfloat16)
+    number = lax.broadcasted_iota(i32, (512, 128), 0)
+    for k in range(8):
+        pair[k : k + 1, :] = pairs[0:1, k * 128 : k * 128 + 128]
+        key = jnp.broadcast_to(pairs[0:1, k * 128 : k * 128 + 128], (512, 128))
+        pair_hot[:, k * 128 : k * 128 + 128] = jnp.where(key == number, 1.0, 0.0).astype(jnp.bfloat16)
+    first = pair[...]
+    held = held_states(pos, vel, rad, first >> 7, first & 127)
+    for c, value in enumerate(held):
+        state[c * 8 : c * 8 + 8, :] = value
+
+
+def held_states(pos, vel, rad, chunk, index):
+    state = []
+    for ref, count in ((pos, 3), (vel, 3), (rad, 1)):
+        for c in range(count):
+            value = jnp.zeros((8, 128), f32)
+            for k in range(4):
+                table = spread(ref[c : c + 1, k * 128 : k * 128 + 128])
+                value = jnp.where(chunk == k, lane_take(table, index), value)
+            state.append(value)
+    return state
+
+
+def stencil_kernel(g, r, pop, ids, low, high, y_low, y_high, forces, hot, base_in, base, sums, shifted, part, left):
     def y_row(c_y, k, x):
         halo = y_low if c_y == 1 else y_high
         if x == -1:
@@ -195,75 +321,45 @@
     def source(direction, x):
         c_x, c_y, c_z = lattice_dirs[direction]
         at = x - c_x
-        if at == -1:
-            k = from_low_x.index(direction)
-            value = low[k * 8 : k * 8 + 8, :]
-        elif at == WX:
-            k = from_high_x.index(direction)
-            value = high[k * 8 : k * 8 + 8, :]
-        else:
-            value = g[direction * ROWS + at * 8 : direction * ROWS + at * 8 + 8, :]
-        if c_y != 0:
-            k = (from_low_y if c_y == 1 else from_high_y).index(direction)
-            value = shift_y(value, c_y, y_row(c_y, k, at))
-        return shift_z(value, c_z)
-
-    combos = [(0, 0), (1, 0), (-1, 0), (0, 1), (0, -1), (1, 1), (-1, -1), (1, -1), (-1, 1)]
+        value = source_plane(g, low, high, direction, at)
+        k = (from_low_y if c_y == 1 else from_high_y).index(direction)
+        return shift_z(shift_y(value, c_y, y_row(c_y, k, at)), c_z)
+
     for at in range(-1, WX + 1):
-        plain = low[40:48, :] if at == -1 else high[40:48, :] if at == WX else r[at * 8 : at * 8 + 8, :]
-        by_y = {0: plain}
+        plain = density_plane(r, low, high, at)
         for c_y in (1, -1):
-            by_y[c_y] = shift_y(plain, c_y, y_row(c_y, None, at))
-        for k, (c_y, c_z) in enumerate(combos):
-            if c_y != 0 and c_z != 0 and not 0 <= at < WX:
-                continue
-            shifted[k * 80 + (at + 1) * 8 : k * 80 + (at + 1) * 8 + 8, :] = shift_z(by_y[c_y], c_z)
+            value = shift_y(plain, c_y, y_row(c_y, None, at))
+            for c_z in (0, 1, -1):
+                if c_z == 0 or 0 <= at < WX:
+                    k = combos.index((c_y, c_z))
+                    shifted[k * 80 + (at + 1) * 8 : k * 80 + (at + 1) * 8 + 8, :] = shift_z(value, c_z)
 
     sub = sublane_iota()
     total = jnp.zeros((160, 128), f32)
     for x in range(WX):
-        rows = slice(x * 8, x * 8 + 8)
-        cell = ids[rows, :]
-        fluid = cell < 0
-        base[x * 8 : x * 8 + 8, :] = jnp.where(fluid, g[x * 8 : x * 8 + 8, :], pop[x * 8 : x * 8 + 8, :])
+        fluid = ids[x * 8 : x * 8 + 8, :] < 0
         acc = [None] * 9
-
-        def add(k, value):
-            acc[k] = value if acc[k] is None else acc[k] + value
-
+        for v in (0, 2, 3, 5, 7):
+            acc[v] = forces[v * ROWS + x * 8 : v * ROWS + x * 8 + 8, :]
+        links = Totals(acc)
         for direction in range(1, 19):
-            vector = lattice_dirs[direction]
-            c_x, c_y, c_z = vector
-            k = combos.index((c_y, c_z))
-            near_r = shifted[k * 80 + (x - c_x + 1) * 8 : k * 80 + (x - c_x + 1) * 8 + 8, :]
+            c_x, c_y, c_z = lattice_dirs[direction]
+            if c_y == 0:
+                continue
+            row = combos.index((c_y, c_z)) * 80 + (x - c_x + 1) * 8
+            near_r = shifted[row : row + 8, :]
             came = source(direction, x)
-            at = direction * ROWS + x * 8
-            back = opposite[direction] * ROWS + x * 8
-            open_link = jnp.where(near_r != 0.0, came, g[back : back + 8, :])
-            base[at : at + 8, :] = jnp.where(fluid, open_link, pop[at : at + 8, :])
-            pull = (-6.0 * lattice_weights[direction]) * near_r
-            for compo in range(3):
-                if vector[compo] == 1:
-                    add(compo, came)
-                elif vector[compo] == -1:
-                    acc[compo] = -came if acc[compo] is None else acc[compo] - came
-                if vector[compo] != 0:
-                    add(3 + compo, pull)
-            for n, (p, q) in enumerate(((0, 1), (0, 2), (1, 2))):
-                if vector[p] * vector[q] == 1:
-                    add(6 + n, pull)
-                elif vector[p] * vector[q] == -1:
-                    acc[6 + n] = -pull if acc[6 + n] is None else acc[6 + n] - pull
+            stream(base, g, pop, fluid, direction, x, came, near_r)
+            links.link(direction, came, near_r)
         for v in range(9):
-            value = 2.0 * acc[v] if v < 3 else acc[v]
+            value = 2.0 * links.acc[v] if v < 3 else links.acc[v]
             head = value.astype(jnp.bfloat16).astype(f32)
             part[v * 8 : v * 8 + 8, :] = head
             part[80 + v * 8 : 80 + v * 8 + 8, :] = value - head
         zero = jnp.zeros((8, 128), f32)
         for y in range(WY):
             key = ids[x * 8 + y : x * 8 + y + 1, :]
-            slot = spread(key & 7)
-            pick = slot == sub
+            pick = spread(key & 7) == sub
             for half in range(2):
                 rows_v = [
                     jnp.where(pick, spread(part[half * 80 + v * 8 + y : half * 80 + v * 8 + y + 1, :]), 0.0)
@@ -272,11 +368,11 @@
                 left[half * 80 : half * 80 + 80, y * 128 : y * 128 + 128] = jnp.concatenate(rows_v, 0).astype(
                     jnp.bfloat16
                 )
-            owner = jnp.broadcast_to(key >> 3, (128, 128))
-            number = lax.broadcasted_iota(i32, (128, 128), 0)
-            hot[:, y * 128 : y * 128 + 128] = jnp.where(owner == number, 1.0, 0.0).astype(jnp.bfloat16)
         total = total + lax.dot_general(
-            left[...], hot[...], (((1,), (1,)), ((), ())), preferred_element_type=f32
+            left[...],
+            hot[:, x * 1024 : x * 1024 + 1024],
+            (((1,), (1,)), ((), ())),
+            preferred_element_type=f32,
         )
     sums[...] = total[0:72, :] + total[80:152, :]
 
@@ -284,16 +380,7 @@
 def reply_kernel(got, pos, vel, rad, sums, out, rows_t):
     rows = got[...].astype(f32).T[0:8, :].astype(i32)
     rows_t[...] = rows
-    chunk = rows >> 7
-    index = rows & 127
-    state = []
-    for ref, count in ((pos, 3), (vel, 3), (rad, 1)):
-        for c in range(count):
-            value = jnp.zeros((8, 128), f32)
-            for k in range(4):
-                table = spread(ref[c : c + 1, k * 128 : k * 128 + 128])
-                value = jnp.where(chunk == k, lane_take(table, index), value)
-            state.append(value)
+    state = held_states(pos, vel, rad, rows >> 7, rows & 127)
     out[pl.ds(0, 128, stride=2), :] = jnp.concatenate(state + [sums[...]], 0).T
     lane = lane_iota()
     side = {-1: (lane & -8) | ((lane - 1) & 7), 1: (lane & -8) | ((lane + 1) & 7)}
@@ -315,9 +402,9 @@
 
 
 def last_kernel(
-    got, rows_t, base, r, ids, low, high, y_low, y_high, pairs, pos, vel, rad, mass,
-    read, vel_next, pos_next,
-    table, around, moving, rim, left, hot, pair,
+    got, rows_t, base, r, ids, low, high, y_low, y_high, pairs, pair_hot, state, pos, vel, mass,
+    read_out, vel_next, pos_next,
+    read, table, around, moving, rim, left, hot, pair, sem,
 ):
     table[...] = got[pl.ds(0, 128, stride=2), :].T
     around[...] = got[pl.ds(1, 128, stride=2), :].T
@@ -376,22 +463,13 @@
             to = direction * ROWS + x * 8
             read[to : to + 8, :] = base[to : to + 8, :] + ((sign * 6.0 * lattice_weights[direction]) * mine) * value
 
+    sent = pltpu.make_async_copy(read, read_out, sem)
+    sent.start()
+
     for k in range(8):
-        pair[k : k + 1, :] = pairs[0:1, k * 128 : k * 128 + 128]
-        pair[8 + k : 9 + k, :] = pairs[1:2, k * 128 : k * 128 + 128]
-    first = pair[0:8, :]
-    second = pair[8:16, :]
-    chunk = first >> 7
-    index = first & 127
-    state_a = []
-    for ref, count in ((pos, 3), (vel, 3), (rad, 1)):
-        for c in range(count):
-            value = jnp.zeros((8, 128), f32)
-            for k in range(4):
-                value = jnp.where(
-                    chunk == k, lane_take(spread(ref[c : c + 1, k * 128 : k * 128 + 128]), index), value
-                )
-            state_a.append(value)
+        pair[k : k + 1, :] = pairs[1:2, k * 128 : k * 128 + 128]
+    second = pair[...]
+    state_a = [state[c * 8 : c * 8 + 8, :] for c in range(7)]
     state_b = look_up(table, tuple(8 * c for c in range(7)), second)
     offset = [a - b for a, b in zip(state_a[0:3], state_b[0:3])]
     length = jnp.sqrt(offset[0] * offset[0] + offset[1] * offset[1] + offset[2] * offset[2])
@@ -414,13 +492,13 @@
         columns = slice(1024 + k * 128, 1024 + k * 128 + 128)
         for c in range(3):
             left[9 + c : 10 + c, columns] = push[c][k : k + 1, :]
-        key = jnp.broadcast_to(pairs[0:1, k * 128 : k * 128 + 128], (512, 128))
-        hot[:, columns] = jnp.where(key == number, 1.0, 0.0).astype(jnp.bfloat16)
     values = left[...]
     head = values.astype(jnp.bfloat16)
     tail = (values - head.astype(f32)).astype(jnp.bfloat16)
-    by_grain = lax.dot_general(
-        jnp.concatenate([head, tail], 0), hot[...], (((1,), (1,)), ((), ())), preferred_element_type=f32
+    both = jnp.concatenate([head, tail], 0)
+    by_grain = lax.dot_general(both[:, 0:1024], hot[...], (((1,), (1,)), ((), ())), preferred_element_type=f32)
+    by_grain = by_grain + lax.dot_general(
+        both[:, 1024:2048], pair_hot[...], (((1,), (1,)), ((), ())), preferred_element_type=f32
     )
     by_grain = by_grain[0:16, :] + by_grain[16:32, :]
     part = [by_grain[n : n + 1, :] for n in range(12)]
@@ -433,6 +511,7 @@
         fresh = speed[c] + (force + part[9 + c]) / mass[...]
         vel_next[c : c + 1, :] = fresh
         pos_next[c : c + 1, :] = pos[c : c + 1, :] + fresh
+    sent.wait()
 
 
 def ring(axis, value, up):
@@ -459,45 +538,59 @@
     ids = cell_grain.reshape(ROWS, 128)
     rad = grain_radius.reshape(1, 512)
     mass = grain_mass.reshape(1, 512)
-    slab = (56, 128)
-    full = (19 * ROWS, 128)
-    g, r, x_up, x_down, y_up, y_down, ask = call(
+    return step(pop, ids, near_rows, contact_pairs, grain_position, grain_velocity, rad, mass)
+
+
+def step(pop, ids, near_rows, contact_pairs, grain_position, grain_velocity, rad, mass):
+    slab = ((56, 128), f32)
+    full = ((19 * ROWS, 128), f32)
+    cells = (ROWS, 128)
+    vector = ((3, 512), f32)
+    scalar = ((1, 512), f32)
+    bf16 = jnp.bfloat16
+    pop, ids, pairs, pos, vel, rad, mass, g, r, x_up, x_down, y_up, y_down, ask = call(
         first_kernel,
-        [(full, f32), ((ROWS, 128), f32), (slab, f32), (slab, f32), (slab, f32), (slab, f32), ((128, 128), i32)],
-    )(pop, ids, near_rows)
+        [full, (cells, i32), ((2, 1024), i32), vector, vector, scalar, scalar]
+        + [full, (cells, f32), slab, slab, slab, slab, ((128, 128), i32)],
+        [pltpu.VMEM((1, 1024), i32), pltpu.VMEM((128, 128), i32), pltpu.SemaphoreType.DMA((9,))],
+        in_specs=[HBM] * 8,
+        out_specs=[VMEM] * 13 + [HBM],
+    )(*[pltpu.with_memory_space_constraint(v, pltpu.HBM) for v in (pop, ids, near_rows, contact_pairs, grain_position, grain_velocity, rad, mass)])
     low = ring("gx", x_up, True)
     high = ring("gx", x_down, False)
     asked = exchange(ask)
     y_up, y_down = call(corner_kernel, [((64, 128), f32), ((64, 128), f32)])(y_up, y_down, low, high)
     y_low = ring("yz", y_up, True)
     y_high = ring("yz", y_down, False)
+    base, forces, hot, pair_hot, state = call(
+        early_kernel,
+        [full, ((9 * ROWS, 128), f32), ((128, 8192), bf16), ((512, 1024), bf16), ((56, 128), f32)],
+        [pltpu.VMEM((240, 128), f32), pltpu.VMEM((8, 128), i32)],
+    )(g, r, pop, ids, low, high, pairs, pos, vel, rad)
     base, sums = call(
         stencil_kernel,
-        [(full, f32), ((72, 128), f32)],
-        [
-            pltpu.VMEM((9 * 80, 128), f32),
-            pltpu.VMEM((160, 128), f32),
-            pltpu.VMEM((160, 1024), jnp.bfloat16),
-            pltpu.VMEM((128, 1024), jnp.bfloat16),
-        ],
-    )(g, r, pop, ids, low, high, y_low, y_high)
-    send, rows_t = call(reply_kernel, [((256, 128), f32), ((8, 128), i32)])(
-        asked, grain_position, grain_velocity, rad, sums
-    )
+        [full, ((72, 128), f32)],
+        [pltpu.VMEM((9 * 80, 128), f32), pltpu.VMEM((160, 128), f32), pltpu.VMEM((160, 1024), bf16)],
+        aliases={10: 0},
+    )(g, r, pop, ids, low, high, y_low, y_high, forces, hot, base)
+    send, rows_t = call(reply_kernel, [((256, 128), f32), ((8, 128), i32)])(asked, pos, vel, rad, sums)
     got = exchange(send.reshape(128, 2, 128)).reshape(256, 128)
     read, vel_next, pos_next = call(
         last_kernel,
-        [(full, f32), ((3, 512), f32), ((3, 512), f32)],
+        [full, vector, vector],
         [
+            pltpu.VMEM((19 * ROWS, 128), f32),
             pltpu.VMEM((128, 128), f32),
             pltpu.VMEM((128, 128), f32),
             pltpu.VMEM((9 * 80, 128), f32),
             pltpu.VMEM((2 * 88, 128), f32),
             pltpu.VMEM((16, 2048), f32),
-            pltpu.VMEM((512, 2048), jnp.bfloat16),
-            pltpu.VMEM((16, 128), i32),
+            pltpu.VMEM((512, 1024), bf16),
+            pltpu.VMEM((8, 128), i32),
+            pltpu.SemaphoreType.DMA,
         ],
-    )(got, rows_t, base, r, ids, low, high, y_low, y_high, contact_pairs, grain_position, grain_velocity, rad, mass)
+        out_specs=[HBM, VMEM, VMEM],
+    )(got, rows_t, base, r, ids, low, high, y_low, y_high, pairs, pair_hot, state, pos, vel, mass)
     return (read.reshape(19, WX, WY, WZ), vel_next, pos_next)
 
 

time: 53.2 us -> 49.6 us (0.932)
  local copies, waits for them, and re-layouts: 3.87 us -> 0 us
  Pallas kernels: 5.35 us -> 7.22 us
  waiting for transfers between devices: 5.15 us -> 3.76 us
    unnamed x20 -> x0, local copies, waits for them, and re-layouts: 3.87 us -> none
    pallas_call x5 -> x6, Pallas kernels: 5.35 us -> 7.22 us  [run(): pl.pallas_call(kernel, out_shape=[jax.ShapeDtypeStruct(s, d) for s, d in...]
    ppermute x4, waiting for transfers between devices: 5.15 us -> 3.76 us  [ring(): return lax.ppermute(value, axis, pairs)]
  transfers between devices with their start and end apart: 5 -> 5, of which waited for: 3 -> 2; matrix products, arithmetic and copies ran while one was open for 0% -> 0% of each run, Pallas kernels for 4% -> 6%
where the time goes in v2:
time: 49.6 us; the launch traced here: 49.5 us
  starting transfers between devices  18.9 us (38%)
  blocking collectives  18.9 us (38%)
  Pallas kernels  7.22 us (15%)
  waiting for transfers between devices  3.76 us (8%)
  between operations  0.69 us (1%)
    all_to_all x1, blocking collectives, exchange(): lax.all_to_all(value, ('gx', 'yz'), split_axis=0, concat_axis=0, tiled=True)  18.9 us
    all_to_all x1, starting transfers between devices, exchange(): lax.all_to_all(value, ('gx', 'yz'), split_axis=0, concat_axis=0, tiled=True)  11.5 us
    ppermute x4, starting transfers between devices, ring(): return lax.ppermute(value, axis, pairs)  7.45 us
    pallas_call x6, Pallas kernels, run(): pl.pallas_call(kernel, out_shape=[jax.ShapeDtypeStruct(s, d) for s, d in...  7.22 us
    ppermute x4, waiting for transfers between devices, ring(): return lax.ppermute(value, axis, pairs)  3.76 us
  transfers between devices with their start and end apart: 5, of which 2 were waited for; matrix products, arithmetic and copies ran while one was open for 0% of the time, Pallas kernels for 6%

profile of v2, /device:TPU:1, one launch (start us, length us, event | category | flops | bytes accessed | tf_op | source)
XLA Modules:
  0.0 49.5 jit_solution(4646332397514812527)
XLA Ops:
  0.6 1.5 %shard_map.103 = (f32[1216,128]{1,0:T(8,128)S(1)}, s32[64,128]{1,0:T(8,128)S(1)}, s32[2,1024]{1,0:T(2,128)S(1)}, f32[3,512]{1,0:T(4,128)S(1)}, f32[3,512]{1,0:T(...) custom-call(f32[1216,128]{1,0:T(8,128)} %bitcast.14, ...), custom_call_target="tpu_custom_call" | custom-call | flops 1000000 | bytes 1048576 | tf_op jit(solution)/shard_map/pallas_call | solution.py:61
  2.2 11.5 %all-to-all-start = ((s32[128,1,128]{2,1,0:T(1,128)}), s32[128,1,128]{2,1,0:T(1,128)S(1)}, u32[]{:S(2)}, u32[]{:S(2)}) async-start(s32[128,1,128]{2,1,0:T(1,128)} %bitcast.5), calls=%async_computation | async-start | bytes 131072 | tf_op jit(solution)/shard_map/all_to_all | solution.py:524
  13.7 1.4 %collective-permute-start = (f32[56,128]{1,0:T(8,128)S(1)}, f32[56,128]{1,0:T(8,128)S(1)}, u32[]{:S(2)}, u32[]{:S(2)}) collective-permute-start(f32[56,128]{1,0:T(8,128)S(1)} %get-tuple-element.39), channel_id=1, source_target_pairs={{0,8},{8,16},{16,24},{24,32},{32,40},{40,48},{48,56},{56,64},{64,7... | collective-permute-start | bytes 86024 | tf_op jit(solution)/shard_map/ppermute | solution.py:520
  15.1 4.1 %collective-permute-start.1 = (f32[56,128]{1,0:T(8,128)S(1)}, f32[56,128]{1,0:T(8,128)S(1)}, u32[]{:S(2)}, u32[]{:S(2)}) collective-permute-start(f32[56,128]{1,0:T(8,128)S(1)} %get-tuple-element.40), channel_id=1, source_target_pairs={{8,0},{16,8},{24,16},{32,24},{40,32},{48,40},{56,48},{64,56},{72,6... | collective-permute-start | bytes 86024 | tf_op jit(solution)/shard_map/ppermute | solution.py:520
  19.2 1.8 %collective-permute-done.low = f32[56,128]{1,0:T(8,128)S(1)} collective-permute-done((f32[56,128]{1,0:T(8,128)S(1)}, f32[56,128]{1,0:T(8,128)S(1)}, u32[]{:S(2)}, u32[]{:S(2)}) %collective-permute-start) | collective-permute-done | bytes 28704 | tf_op jit(solution)/shard_map/ppermute | solution.py:520
  21.0 0.0 collective-permute-done.1.high
  21.0 1.9 %collective-permute-start.2 = (f32[64,128]{1,0:T(8,128)S(1)}, f32[64,128]{1,0:T(8,128)S(1)}, u32[]{:S(2)}, u32[]{:S(2)}) collective-permute-start(f32[64,128]{1,0:T(8,128)S(1)} %get-tuple-element.43), channel_id=1, source_target_pairs={{0,1},{1,2},{2,3},{3,4},{4,5},{5,6},{6,7},{7,0},{8,9},{9,10},{10,1... | collective-permute-start | bytes 98312 | tf_op jit(solution)/shard_map/ppermute | solution.py:520
  22.9 0.0 collective-permute-start.3
  22.9 1.4 %shard_map.105 = (f32[1216,128]{1,0:T(8,128)S(1)}, f32[576,128]{1,0:T(8,128)S(1)}, bf16[128,8192]{1,0:T(8,128)(2,1)S(1)}, bf16[512,1024]{1,0:T(8,128)(2,1)S(1)}, f32[56,128]{1,0:T(8,128)S(1)}) custom-call(f32[1216,128]{1,0:T(8,128)S(1)} %get-tuple-element.35.g, f32[64,128]{1,0:T(8,128)S(1)} %get-tuple-element.36.r, f32[1216,128]{1,0:T(8,128)S(1)} %get-tuple-element.37.pop, ...), custom_call_target="tpu_custom_call" | custom-call | flops 1000000 | bytes 1048576 | tf_op jit(solution)/shard_map/pallas_call | solution.py:61
  24.3 0.0 collective-permute-done.2.y_low
  24.3 1.9 %collective-permute-done.3.y_high = f32[64,128]{1,0:T(8,128)S(1)} collective-permute-done((f32[64,128]{1,0:T(8,128)S(1)}, f32[64,128]{1,0:T(8,128)S(1)}, u32[]{:S(2)}, u32[]{:S(2)}) %collective-permute-start.3) | collective-permute-done | bytes 32800 | tf_op jit(solution)/shard_map/ppermute | solution.py:520
  26.3 1.5 %shard_map.106 = (f32[1216,128]{1,0:T(8,128)S(1)}, f32[72,128]{1,0:T(8,128)S(1)}) custom-call(f32[1216,128]{1,0:T(8,128)S(1)} %get-tuple-element.35.g, f32[64,128]{1,0:T(8,128)S(1)} %get-tuple-element.36.r, f32[1216,128]{1,0:T(8,128)S(1)} %get-tuple-element.37.pop, s32[64,128]{1,0:T(8,128)S(1)} %get-tuple-element.38.ids, ...), custom_call_target="tpu_custom_call", output_to_operand_aliasing={{0}: (10, {})} | custom-call | flops 1000000 | bytes 1048576 | tf_op jit(solution)/shard_map/pallas_call | solution.py:61
  27.8 0.0 all-to-all-done
  27.8 0.4 shard_map.107
  28.2 18.9 %all_to_all.16 = f32[128,2,128]{2,1,0:T(2,128)S(1)} all-to-all(f32[128,2,128]{2,1,0:T(2,128)S(1)} %bitcast.13), channel_id=1, replica_groups=mesh['gx'=16,'yz'=8] {'gx','yz'}, dimensions={0} | all-to-all | bytes 262144 | tf_op jit(solution)/shard_map/all_to_all | solution.py:524
  47.0 2.5 %shard_map.108 = (f32[1216,128]{1,0:T(8,128)}, f32[3,512]{1,0:T(4,128)}, f32[3,512]{1,0:T(4,128)}) custom-call(f32[256,128]{1,0:T(8,128)S(1)} %bitcast.11, s32[8,128]{1,0:T(8,128)S(1)} %get-tuple-element.51.rows_t, f32[1216,128]{1,0:T(8,128)S(1)} %get-tuple-element.52.base, f32[64,128]{1,0:T(8,128)S(1)} %get-tuple-element.36.r, ...), custom_call_target="tpu_custom_call" | custom-call | flops 1000000 | bytes 1048576 | tf_op jit(solution)/shard_map/pallas_call | solution.py:61
  (1 shorter events, 0.0 us)
Async XLA Ops:
  2.2 25.6 %all-to-all-start = ((s32[128,1,128]{2,1,0:T(1,128)}), s32[128,1,128]{2,1,0:T(1,128)S(1)}, u32[]{:S(2)}, u32[]{:S(2)}) async-start(s32[128,1,128]{2,1,0:T(1,128)} %bitcast.5), calls=%async_computation | async-start | bytes 131072 | tf_op jit(solution)/shard_map/all_to_all | solution.py:524
  13.7 7.3 %collective-permute-start = (f32[56,128]{1,0:T(8,128)S(1)}, f32[56,128]{1,0:T(8,128)S(1)}, u32[]{:S(2)}, u32[]{:S(2)}) collective-permute-start(f32[56,128]{1,0:T(8,128)S(1)} %get-tuple-element.39), channel_id=1, source_target_pairs={{0,8},{8,16},{16,24},{24,32},{32,40},{40,48},{48,56},{56,64},{64,7... | collective-permute-start | bytes 86024 | tf_op jit(solution)/shard_map/ppermute | solution.py:520
  15.1 5.9 %collective-permute-start.1 = (f32[56,128]{1,0:T(8,128)S(1)}, f32[56,128]{1,0:T(8,128)S(1)}, u32[]{:S(2)}, u32[]{:S(2)}) collective-permute-start(f32[56,128]{1,0:T(8,128)S(1)} %get-tuple-element.40), channel_id=1, source_target_pairs={{8,0},{16,8},{24,16},{32,24},{40,32},{48,40},{56,48},{64,56},{72,6... | collective-permute-start | bytes 86024 | tf_op jit(solution)/shard_map/ppermute | solution.py:520
  21.0 3.3 %collective-permute-start.2 = (f32[64,128]{1,0:T(8,128)S(1)}, f32[64,128]{1,0:T(8,128)S(1)}, u32[]{:S(2)}, u32[]{:S(2)}) collective-permute-start(f32[64,128]{1,0:T(8,128)S(1)} %get-tuple-element.43), channel_id=1, source_target_pairs={{0,1},{1,2},{2,3},{3,4},{4,5},{5,6},{6,7},{7,0},{8,9},{9,10},{10,1... | collective-permute-start | bytes 98312 | tf_op jit(solution)/shard_map/ppermute | solution.py:520
  22.9 3.3 %collective-permute-start.3 = (f32[64,128]{1,0:T(8,128)S(1)}, f32[64,128]{1,0:T(8,128)S(1)}, u32[]{:S(2)}, u32[]{:S(2)}) collective-permute-start(f32[64,128]{1,0:T(8,128)S(1)} %get-tuple-element.44), channel_id=1, source_target_pairs={{1,0},{2,1},{3,2},{4,3},{5,4},{6,5},{7,6},{0,7},{9,8},{10,9},{11,1... | collective-permute-start | bytes 98312 | tf_op jit(solution)/shard_map/ppermute | solution.py:520

commit v3 on v2

--- a/solution.py
+++ b/solution.py
@@ -134,36 +134,38 @@
     pop, ids, pairs, pos, vel, rad, mass, g, r, x_up, x_down, y_up, y_down, ask_out,
     near, ask, sems,
 ):
-    copies = [
-        pltpu.make_async_copy(src, dst, sems.at[k])
+    def copy(k, src, dst):
+        started = pltpu.make_async_copy(src, dst, sems.at[k])
+        started.start()
+        return started
+
+    asking = copy(0, near_in, near)
+    cells = copy(1, ids_in, ids)
+    planes = ((0, WX - 1), (1, 2), (3, 4), (5, 6))
+    arriving = [
+        [copy(2 + 2 * n + m, pop_in.at[:, x], pop.at[:, x]) for m, x in enumerate(chunk)]
+        for n, chunk in enumerate(planes)
+    ]
+    others = [
+        copy(10 + k, src, dst)
         for k, (src, dst) in enumerate(
-            (
-                (near_in, near),
-                (ids_in, ids),
-                (pop_in, pop),
-                (pairs_in, pairs),
-                (pos_in, pos),
-                (vel_in, vel),
-                (rad_in, rad),
-                (mass_in, mass),
-            )
+            ((pairs_in, pairs), (pos_in, pos), (vel_in, vel), (rad_in, rad), (mass_in, mass))
         )
     ]
-    for copy in copies:
-        copy.start()
-    copies[0].wait()
+    asking.wait()
     lane = lane_iota()
     sub = sublane_iota()
     for tile in range(16):
         row = near[0:1, (tile // 2) * 128 : (tile // 2) * 128 + 128]
         index = (8 * (tile % 2) + sub) * 8 + (lane & 7)
         ask[tile * 8 : tile * 8 + 8, :] = lane_take(spread(row), index)
-    sent = pltpu.make_async_copy(ask, ask_out, sems.at[8])
-    sent.start()
-    copies[1].wait()
-    copies[2].wait()
-    for x in range(WX):
-        pops = [pop[c * ROWS + x * 8 : c * ROWS + x * 8 + 8, :] for c in range(19)]
+    sent = copy(15, ask, ask_out)
+    cells.wait()
+    for n, x in ((n, x) for n, chunk in enumerate(planes) for x in chunk):
+        if x == planes[n][0]:
+            for arrival in arriving[n]:
+                arrival.wait()
+        pops = [pop[c, x] for c in range(19)]
         cell = ids[x * 8 : x * 8 + 8, :]
         fluid = cell < 0
         post, total = collide(pops)
@@ -183,8 +185,8 @@
             out[k * 8 : k * 8 + 8, :] = g[pl.ds(c * ROWS + y, 8, stride=8), :]
         out[40:48, :] = r[pl.ds(y, 8, stride=8), :]
         out[48:56, :] = ids[pl.ds(y, 8, stride=8), :].astype(f32)
-    for copy in copies[3:]:
-        copy.wait()
+    for other in others:
+        other.wait()
     sent.wait()
 
 
@@ -238,13 +240,6 @@
                 self.add(6 + n, pull, vector[p] * vector[q])
 
 
-def stream(base, g, pop, fluid, direction, x, came, near_r):
-    at = direction * ROWS + x * 8
-    back = opposite[direction] * ROWS + x * 8
-    open_link = jnp.where(near_r != 0.0, came, g[back : back + 8, :])
-    base[at : at + 8, :] = jnp.where(fluid, open_link, pop[at : at + 8, :])
-
-
 def source_plane(g, low, high, direction, at):
     if at == -1:
         k = from_low_x.index(direction)
@@ -259,40 +254,117 @@
     return low[40:48, :] if at == -1 else high[40:48, :] if at == WX else r[at * 8 : at * 8 + 8, :]
 
 
-def early_kernel(g, r, pop, ids, low, high, pairs, pos, vel, rad, base, forces, hot, pair_hot, state, shifted, pair):
+def spread_slots(part, row, pick):
+    halves = []
+    for half in range(2):
+        rows_v = [
+            jnp.where(pick, spread(part[half * 72 + v * 8 + row : half * 72 + v * 8 + row + 1, :]), 0.0) for v in range(9)
+        ]
+        halves.append(jnp.concatenate(rows_v + [jnp.zeros((8, 128), f32)], 0).astype(jnp.bfloat16))
+    return jnp.concatenate(halves, 0)
+
+
+def split_fields(part, acc):
+    for v in range(9):
+        if acc[v] is None:
+            part[v * 8 : v * 8 + 8, :] = jnp.zeros((8, 128), f32)
+            part[72 + v * 8 : 80 + v * 8, :] = jnp.zeros((8, 128), f32)
+            continue
+        value = 2.0 * acc[v] if v < 3 else acc[v]
+        head = value.astype(jnp.bfloat16).astype(f32)
+        part[v * 8 : v * 8 + 8, :] = head
+        part[72 + v * 8 : 80 + v * 8, :] = value - head
+
+
+def contract(left, right):
+    return lax.dot_general(left, right, (((1,), (1,)), ((), ())), preferred_element_type=f32)
+
+
+def early_kernel(
+    g, r, pop, ids, low, high, pairs, pos, vel, rad,
+    base, sums, edge_hot, pair_hot, state,
+    shifted, part, left, hot, pair,
+):
+    sub = sublane_iota()
+
+    def shift(value, c_y, c_z):
+        if c_y == 1:
+            value = jnp.where(sub == 0, 0.0, pltpu.roll(value, 1, 0))
+        elif c_y == -1:
+            value = jnp.where(sub == WY - 1, 0.0, pltpu.roll(value, WY - 1, 0))
+        return shift_z(value, c_z)
+
     for at in range(-1, WX + 1):
         plain = density_plane(r, low, high, at)
-        for k, c_z in enumerate((0, 1, -1)):
-            shifted[k * 80 + (at + 1) * 8 : k * 80 + (at + 1) * 8 + 8, :] = shift_z(plain, c_z)
+        for k, (c_y, c_z) in enumerate(combos):
+            if 0 <= at < WX or c_y == 0 or c_z == 0:
+                shifted[k * 80 + (at + 1) * 8 : k * 80 + (at + 1) * 8 + 8, :] = shift(plain, c_y, c_z)
+    number = lax.broadcasted_iota(i32, (128, 128), 0)
+    total = jnp.zeros((160, 128), f32)
     for x in range(WX):
         fluid = ids[x * 8 : x * 8 + 8, :] < 0
         base[x * 8 : x * 8 + 8, :] = jnp.where(fluid, g[x * 8 : x * 8 + 8, :], pop[x * 8 : x * 8 + 8, :])
-        sums = Totals()
+        links = Totals()
         for direction in range(1, 19):
             c_x, c_y, c_z = lattice_dirs[direction]
-            if c_y != 0:
-                continue
-            at = x - c_x
-            row = (0, 1, -1).index(c_z) * 80 + (at + 1) * 8
+            row = combos.index((c_y, c_z)) * 80 + (x - c_x + 1) * 8
             near_r = shifted[row : row + 8, :]
-            came = shift_z(source_plane(g, low, high, direction, at), c_z)
-            stream(base, g, pop, fluid, direction, x, came, near_r)
-            sums.link(direction, came, near_r)
-        for v in (0, 2, 3, 5, 7):
-            forces[v * ROWS + x * 8 : v * ROWS + x * 8 + 8, :] = sums.acc[v]
-    number = lax.broadcasted_iota(i32, (128, 128), 0)
-    for row in range(ROWS):
-        owner = jnp.broadcast_to(ids[row : row + 1, :] >> 3, (128, 128))
-        hot[:, row * 128 : row * 128 + 128] = jnp.where(owner == number, 1.0, 0.0).astype(jnp.bfloat16)
-    number = lax.broadcasted_iota(i32, (512, 128), 0)
+            came = shift(source_plane(g, low, high, direction, x - c_x), c_y, c_z)
+            at = direction * ROWS + x * 8
+            back = opposite[direction] * ROWS + x * 8
+            open_link = jnp.where(near_r != 0.0, came, g[back : back + 8, :])
+            base[at : at + 8, :] = jnp.where(fluid, open_link, pop[at : at + 8, :])
+            links.link(direction, came, near_r)
+        split_fields(part, links.acc)
+        for y in range(WY):
+            key = ids[x * 8 + y : x * 8 + y + 1, :]
+            left[:, y * 128 : y * 128 + 128] = spread_slots(part, y, spread(key & 7) == sub)
+            owner = jnp.broadcast_to(key >> 3, (128, 128))
+            one_hot = jnp.where(owner == number, 1.0, 0.0).astype(jnp.bfloat16)
+            hot[:, y * 128 : y * 128 + 128] = one_hot
+            if y in (0, WY - 1):
+                to = (0 if y == 0 else 1024) + x * 128
+                edge_hot[:, to : to + 128] = one_hot
+        total = total + contract(left[...], hot[...])
+    sums[...] = total[0:72, :] + total[80:152, :]
     for k in range(8):
-        pair[k : k + 1, :] = pairs[0:1, k * 128 : k * 128 + 128]
-        key = jnp.broadcast_to(pairs[0:1, k * 128 : k * 128 + 128], (512, 128))
-        pair_hot[:, k * 128 : k * 128 + 128] = jnp.where(key == number, 1.0, 0.0).astype(jnp.bfloat16)
+        key = pairs[0:1, k * 128 : k * 128 + 128]
+        pair[k : k + 1, :] = key
+        rest = jnp.broadcast_to(key & 127, (128, 128))
+        pair_hot[:, k * 128 : k * 128 + 128] = jnp.where(rest == number, 1.0, 0.0).astype(jnp.bfloat16)
     first = pair[...]
     held = held_states(pos, vel, rad, first >> 7, first & 127)
     for c, value in enumerate(held):
         state[c * 8 : c * 8 + 8, :] = value
+
+
+def complete_rows(ids, y_low, y_high, edge_hot, base, part, left):
+    sub = sublane_iota()
+    total = jnp.zeros((160, 128), f32)
+    for side, (y, halo, names) in enumerate(((0, y_low, from_low_y), (WY - 1, y_high, from_high_y))):
+        fluid = ids[pl.ds(y, 8, stride=8), :] < 0
+        links = Totals()
+        for k, direction in enumerate(names):
+            c_x, _, c_z = lattice_dirs[direction]
+            came = halo[k * 8 : k * 8 + 8, :]
+            near_r = halo[40:48, :]
+            if c_x == 1:
+                came = jnp.where(sub == 0, spread(halo[56:57, :]), pltpu.roll(came, 1, 0))
+                near_r = jnp.where(sub == 0, spread(halo[57:58, :]), pltpu.roll(near_r, 1, 0))
+            elif c_x == -1:
+                came = jnp.where(sub == WX - 1, spread(halo[59:60, :]), pltpu.roll(came, WX - 1, 0))
+                near_r = jnp.where(sub == WX - 1, spread(halo[60:61, :]), pltpu.roll(near_r, WX - 1, 0))
+            came = shift_z(came, c_z)
+            near_r = shift_z(near_r, c_z)
+            at = pl.ds(direction * ROWS + y, 8, stride=8)
+            base[at, :] = jnp.where(fluid & (near_r != 0.0), came, base[at, :])
+            links.link(direction, came, near_r)
+        split_fields(part, links.acc)
+        for x in range(WX):
+            key = ids[x * 8 + y : x * 8 + y + 1, :]
+            left[:, x * 128 : x * 128 + 128] = spread_slots(part, x, spread(key & 7) == sub)
+        total = total + contract(left[...], edge_hot[:, side * 1024 : side * 1024 + 1024])
+    return total[0:72, :] + total[80:152, :]
 
 
 def held_states(pos, vel, rad, chunk, index):
@@ -307,81 +379,14 @@
     return state
 
 
-def stencil_kernel(g, r, pop, ids, low, high, y_low, y_high, forces, hot, base_in, base, sums, shifted, part, left):
-    def y_row(c_y, k, x):
-        halo = y_low if c_y == 1 else y_high
-        if x == -1:
-            at = 56 + (1 if k is None else 0)
-        elif x == WX:
-            at = 59 + (1 if k is None else 0)
-        else:
-            at = (5 if k is None else k) * 8 + x
-        return halo[at : at + 1, :]
-
-    def source(direction, x):
-        c_x, c_y, c_z = lattice_dirs[direction]
-        at = x - c_x
-        value = source_plane(g, low, high, direction, at)
-        k = (from_low_y if c_y == 1 else from_high_y).index(direction)
-        return shift_z(shift_y(value, c_y, y_row(c_y, k, at)), c_z)
-
-    for at in range(-1, WX + 1):
-        plain = density_plane(r, low, high, at)
-        for c_y in (1, -1):
-            value = shift_y(plain, c_y, y_row(c_y, None, at))
-            for c_z in (0, 1, -1):
-                if c_z == 0 or 0 <= at < WX:
-                    k = combos.index((c_y, c_z))
-                    shifted[k * 80 + (at + 1) * 8 : k * 80 + (at + 1) * 8 + 8, :] = shift_z(value, c_z)
-
-    sub = sublane_iota()
-    total = jnp.zeros((160, 128), f32)
-    for x in range(WX):
-        fluid = ids[x * 8 : x * 8 + 8, :] < 0
-        acc = [None] * 9
-        for v in (0, 2, 3, 5, 7):
-            acc[v] = forces[v * ROWS + x * 8 : v * ROWS + x * 8 + 8, :]
-        links = Totals(acc)
-        for direction in range(1, 19):
-            c_x, c_y, c_z = lattice_dirs[direction]
-            if c_y == 0:
-                continue
-            row = combos.index((c_y, c_z)) * 80 + (x - c_x + 1) * 8
-            near_r = shifted[row : row + 8, :]
-            came = source(direction, x)
-            stream(base, g, pop, fluid, direction, x, came, near_r)
-            links.link(direction, came, near_r)
-        for v in range(9):
-            value = 2.0 * links.acc[v] if v < 3 else links.acc[v]
-            head = value.astype(jnp.bfloat16).astype(f32)
-            part[v * 8 : v * 8 + 8, :] = head
-            part[80 + v * 8 : 80 + v * 8 + 8, :] = value - head
-        zero = jnp.zeros((8, 128), f32)
-        for y in range(WY):
-            key = ids[x * 8 + y : x * 8 + y + 1, :]
-            pick = spread(key & 7) == sub
-            for half in range(2):
-                rows_v = [
-                    jnp.where(pick, spread(part[half * 80 + v * 8 + y : half * 80 + v * 8 + y + 1, :]), 0.0)
-                    for v in range(9)
-                ] + [zero]
-                left[half * 80 : half * 80 + 80, y * 128 : y * 128 + 128] = jnp.concatenate(rows_v, 0).astype(
-                    jnp.bfloat16
-                )
-        total = total + lax.dot_general(
-            left[...],
-            hot[:, x * 1024 : x * 1024 + 1024],
-            (((1,), (1,)), ((), ())),
-            preferred_element_type=f32,
-        )
-    sums[...] = total[0:72, :] + total[80:152, :]
-
-
-def reply_kernel(got, pos, vel, rad, sums, out, rows_t):
+def reply_kernel(
+    got, pos, vel, rad, sums, ids, y_low, y_high, edge_hot, base_in, out, rows_t, base, part, left
+):
+    sums = sums[...] + complete_rows(ids, y_low, y_high, edge_hot, base, part, left)
     rows = got[...].astype(f32).T[0:8, :].astype(i32)
     rows_t[...] = rows
     state = held_states(pos, vel, rad, rows >> 7, rows & 127)
-    out[pl.ds(0, 128, stride=2), :] = jnp.concatenate(state + [sums[...]], 0).T
+    out[pl.ds(0, 128, stride=2), :] = jnp.concatenate(state + [sums], 0).T
     lane = lane_iota()
     side = {-1: (lane & -8) | ((lane - 1) & 7), 1: (lane & -8) | ((lane + 1) & 7)}
 
@@ -401,24 +406,25 @@
     out[pl.ds(1, 128, stride=2), :] = jnp.concatenate(rest, 0).T
 
 
+def look_up(ref, starts, cell):
+    owner = (cell >> 3) & 127
+    slot = jnp.where(cell >= 0, cell & 7, 8)
+    values = [jnp.zeros((8, 128), f32) for start in starts]
+    for s in range(8):
+        chosen = slot == s
+        for n, start in enumerate(starts):
+            taken = lane_take(spread(ref[start + s : start + s + 1, :]), owner)
+            values[n] = jnp.where(chosen, taken, values[n])
+    return values
+
+
 def last_kernel(
     got, rows_t, base, r, ids, low, high, y_low, y_high, pairs, pair_hot, state, pos, vel, mass,
-    read_out, vel_next, pos_next,
-    read, table, around, moving, rim, left, hot, pair, sem,
+    read_out, vel_out, pos_out,
+    read, vel_next, pos_next, table, around, moving, rim, left, hot, pair, sems,
 ):
     table[...] = got[pl.ds(0, 128, stride=2), :].T
     around[...] = got[pl.ds(1, 128, stride=2), :].T
-
-    def look_up(ref, starts, cell):
-        owner = (cell >> 3) & 127
-        slot = jnp.where(cell >= 0, cell & 7, 8)
-        values = [jnp.zeros((8, 128), f32) for start in starts]
-        for s in range(8):
-            chosen = slot == s
-            for n, start in enumerate(starts):
-                taken = lane_take(spread(ref[start + s : start + s + 1, :]), owner)
-                values[n] = jnp.where(chosen, taken, values[n])
-        return values
 
     def combine(values, vector):
         total = None
@@ -463,9 +469,22 @@
             to = direction * ROWS + x * 8
             read[to : to + 8, :] = base[to : to + 8, :] + ((sign * 6.0 * lattice_weights[direction]) * mine) * value
 
-    sent = pltpu.make_async_copy(read, read_out, sem)
+    sent = pltpu.make_async_copy(read, read_out, sems.at[0])
     sent.start()
 
+    @pl.when(lax.axis_index("gx") >= 0)
+    def _():
+        grains(rows_t, pairs, pair_hot, state, pos, vel, mass, vel_next, pos_next, table, left, hot, pair)
+
+    outs = [pltpu.make_async_copy(vel_next, vel_out, sems.at[1]), pltpu.make_async_copy(pos_next, pos_out, sems.at[2])]
+    for out in outs:
+        out.start()
+    for out in outs:
+        out.wait()
+    sent.wait()
+
+
+def grains(rows_t, pairs, pair_hot, state, pos, vel, mass, vel_next, pos_next, table, left, hot, pair):
     for k in range(8):
         pair[k : k + 1, :] = pairs[1:2, k * 128 : k * 128 + 128]
     second = pair[...]
@@ -482,36 +501,45 @@
     size = stiffness * inter - damping * inter * closing
     push = [size * n for n in normal]
 
-    left[...] = jnp.zeros((16, 2048), f32)
-    number = lax.broadcasted_iota(i32, (512, 128), 0)
+    sub = sublane_iota()
+    number = lax.broadcasted_iota(i32, (128, 128), 0)
+
+    def by_block(values, key):
+        pick = spread(key >> 7) == (sub & 3)
+        tiles = ([], [])
+        for n in range(0, len(values), 2):
+            value = spread(values[n])
+            if n + 1 < len(values):
+                value = jnp.where(sub < 4, value, spread(values[n + 1]))
+            value = jnp.where(pick, value, 0.0)
+            head = value.astype(jnp.bfloat16).astype(f32)
+            tiles[0].append(head)
+            tiles[1].append(value - head)
+        return jnp.concatenate(tiles[0] + tiles[1], 0).astype(jnp.bfloat16)
+
     for s in range(8):
-        left[0:9, s * 128 : s * 128 + 128] = table[pl.ds(56 + s, 9, stride=8), :]
-        key = jnp.broadcast_to(rows_t[s : s + 1, :], (512, 128))
-        hot[:, s * 128 : s * 128 + 128] = jnp.where(key == number, 1.0, 0.0).astype(jnp.bfloat16)
-    for k in range(8):
-        columns = slice(1024 + k * 128, 1024 + k * 128 + 128)
+        columns = slice(s * 128, s * 128 + 128)
+        key = rows_t[s : s + 1, :]
+        left[0:80, columns] = by_block([table[56 + v * 8 + s : 57 + v * 8 + s, :] for v in range(9)], key)
+        rest = jnp.broadcast_to(jnp.where(key >= 0, key & 127, -1), (128, 128))
+        hot[:, columns] = jnp.where(rest == number, 1.0, 0.0).astype(jnp.bfloat16)
+        left[80:112, columns] = by_block([p[s : s + 1, :] for p in push], pairs[0:1, columns])
+    fluid = contract(left[0:80, :], hot[...])
+    fluid = fluid[0:40, :] + fluid[40:80, :]
+    contact = contract(left[80:112, :], pair_hot[...])
+    contact = contact[0:16, :] + contact[16:32, :]
+    matrix = ((3, 6, 7), (6, 4, 8), (7, 8, 5))
+    for k in range(4):
+        columns = slice(k * 128, k * 128 + 128)
+        speed = [vel[c : c + 1, columns] for c in range(3)]
         for c in range(3):
-            left[9 + c : 10 + c, columns] = push[c][k : k + 1, :]
-    values = left[...]
-    head = values.astype(jnp.bfloat16)
-    tail = (values - head.astype(f32)).astype(jnp.bfloat16)
-    both = jnp.concatenate([head, tail], 0)
-    by_grain = lax.dot_general(both[:, 0:1024], hot[...], (((1,), (1,)), ((), ())), preferred_element_type=f32)
-    by_grain = by_grain + lax.dot_general(
-        both[:, 1024:2048], pair_hot[...], (((1,), (1,)), ((), ())), preferred_element_type=f32
-    )
-    by_grain = by_grain[0:16, :] + by_grain[16:32, :]
-    part = [by_grain[n : n + 1, :] for n in range(12)]
-    speed = [vel[c : c + 1, :] for c in range(3)]
-    matrix = ((3, 6, 7), (6, 4, 8), (7, 8, 5))
-    for c in range(3):
-        force = part[c]
-        for q in range(3):
-            force = force + part[matrix[c][q]] * speed[q]
-        fresh = speed[c] + (force + part[9 + c]) / mass[...]
-        vel_next[c : c + 1, :] = fresh
-        pos_next[c : c + 1, :] = pos[c : c + 1, :] + fresh
-    sent.wait()
+            force = fluid[c * 4 + k : c * 4 + k + 1, :]
+            for q in range(3):
+                row = matrix[c][q] * 4 + k
+                force = force + fluid[row : row + 1, :] * speed[q]
+            fresh = speed[c] + (force + contact[c * 4 + k : c * 4 + k + 1, :]) / mass[:, columns]
+            vel_next[c : c + 1, columns] = fresh
+            pos_next[c : c + 1, columns] = pos[c : c + 1, columns] + fresh
 
 
 def ring(axis, value, up):
@@ -534,7 +562,7 @@
     grain_radius,
     grain_mass,
 ):
-    pop = populations.reshape(19 * ROWS, 128)
+    pop = populations
     ids = cell_grain.reshape(ROWS, 128)
     rad = grain_radius.reshape(1, 512)
     mass = grain_mass.reshape(1, 512)
@@ -550,46 +578,59 @@
     bf16 = jnp.bfloat16
     pop, ids, pairs, pos, vel, rad, mass, g, r, x_up, x_down, y_up, y_down, ask = call(
         first_kernel,
-        [full, (cells, i32), ((2, 1024), i32), vector, vector, scalar, scalar]
+        [((19, WX, WY, WZ), f32), (cells, i32), ((2, 1024), i32), vector, vector, scalar, scalar]
         + [full, (cells, f32), slab, slab, slab, slab, ((128, 128), i32)],
-        [pltpu.VMEM((1, 1024), i32), pltpu.VMEM((128, 128), i32), pltpu.SemaphoreType.DMA((9,))],
+        [pltpu.VMEM((1, 1024), i32), pltpu.VMEM((128, 128), i32), pltpu.SemaphoreType.DMA((16,))],
         in_specs=[HBM] * 8,
         out_specs=[VMEM] * 13 + [HBM],
-    )(*[pltpu.with_memory_space_constraint(v, pltpu.HBM) for v in (pop, ids, near_rows, contact_pairs, grain_position, grain_velocity, rad, mass)])
+    )(
+        *[
+            pltpu.with_memory_space_constraint(value, pltpu.HBM)
+            for value in (pop, ids, near_rows, contact_pairs, grain_position, grain_velocity, rad, mass)
+        ]
+    )
+    pop = pop.reshape(19 * ROWS, 128)
     low = ring("gx", x_up, True)
     high = ring("gx", x_down, False)
     asked = exchange(ask)
     y_up, y_down = call(corner_kernel, [((64, 128), f32), ((64, 128), f32)])(y_up, y_down, low, high)
     y_low = ring("yz", y_up, True)
     y_high = ring("yz", y_down, False)
-    base, forces, hot, pair_hot, state = call(
+    base, sums, edge_hot, pair_hot, state = call(
         early_kernel,
-        [full, ((9 * ROWS, 128), f32), ((128, 8192), bf16), ((512, 1024), bf16), ((56, 128), f32)],
-        [pltpu.VMEM((240, 128), f32), pltpu.VMEM((8, 128), i32)],
+        [full, ((72, 128), f32), ((128, 2048), bf16), ((128, 1024), bf16), ((56, 128), f32)],
+        [
+            pltpu.VMEM((9 * 80, 128), f32),
+            pltpu.VMEM((144, 128), f32),
+            pltpu.VMEM((160, 1024), bf16),
+            pltpu.VMEM((128, 1024), bf16),
+            pltpu.VMEM((8, 128), i32),
+        ],
     )(g, r, pop, ids, low, high, pairs, pos, vel, rad)
-    base, sums = call(
-        stencil_kernel,
-        [full, ((72, 128), f32)],
-        [pltpu.VMEM((9 * 80, 128), f32), pltpu.VMEM((160, 128), f32), pltpu.VMEM((160, 1024), bf16)],
-        aliases={10: 0},
-    )(g, r, pop, ids, low, high, y_low, y_high, forces, hot, base)
-    send, rows_t = call(reply_kernel, [((256, 128), f32), ((8, 128), i32)])(asked, pos, vel, rad, sums)
+    send, rows_t, base = call(
+        reply_kernel,
+        [((256, 128), f32), ((8, 128), i32), full],
+        [pltpu.VMEM((144, 128), f32), pltpu.VMEM((160, 1024), bf16)],
+        aliases={9: 2},
+    )(asked, pos, vel, rad, sums, ids, y_low, y_high, edge_hot, base)
     got = exchange(send.reshape(128, 2, 128)).reshape(256, 128)
     read, vel_next, pos_next = call(
         last_kernel,
         [full, vector, vector],
         [
             pltpu.VMEM((19 * ROWS, 128), f32),
+            pltpu.VMEM((3, 512), f32),
+            pltpu.VMEM((3, 512), f32),
             pltpu.VMEM((128, 128), f32),
             pltpu.VMEM((128, 128), f32),
             pltpu.VMEM((9 * 80, 128), f32),
             pltpu.VMEM((2 * 88, 128), f32),
-            pltpu.VMEM((16, 2048), f32),
-            pltpu.VMEM((512, 1024), bf16),
+            pltpu.VMEM((112, 1024), bf16),
+            pltpu.VMEM((128, 1024), bf16),
             pltpu.VMEM((8, 128), i32),
-            pltpu.SemaphoreType.DMA,
+            pltpu.SemaphoreType.DMA((3,)),
         ],
-        out_specs=[HBM, VMEM, VMEM],
+        out_specs=[HBM] * 3,
     )(got, rows_t, base, r, ids, low, high, y_low, y_high, pairs, pair_hot, state, pos, vel, mass)
     return (read.reshape(19, WX, WY, WZ), vel_next, pos_next)
 

time: 49.6 us -> 47.7 us (0.962)
  Pallas kernels: 7.22 us -> 6.17 us
  waiting for transfers between devices: 3.76 us -> 2.84 us
    pallas_call x6 -> x5, Pallas kernels: 7.22 us -> 6.17 us  [run(): pl.pallas_call(kernel, out_shape=[jax.ShapeDtypeStruct(s, d) for s, d in...]
    ppermute x4, waiting for transfers between devices: 3.76 us -> 2.84 us  [ring(): return lax.ppermute(value, axis, pairs)]
  transfers between devices with their start and end apart: 5 -> 5, of which waited for: 2 -> 2; matrix products, arithmetic and copies ran while one was open for 0% -> 0% of each run, Pallas kernels for 6% -> 5%
where the time goes in v3:
time: 47.7 us; the launch traced here: 47.5 us
  starting transfers between devices  18.9 us (40%)
  blocking collectives  18.8 us (39%)
  Pallas kernels  6.17 us (13%)
  waiting for transfers between devices  2.84 us (6%)
  between operations  0.67 us (1%)
    all_to_all x1, blocking collectives, exchange(): lax.all_to_all(value, ('gx', 'yz'), split_axis=0, concat_axis=0, tiled=True)  18.8 us
    all_to_all x1, starting transfers between devices, exchange(): lax.all_to_all(value, ('gx', 'yz'), split_axis=0, concat_axis=0, tiled=True)  11.5 us
    ppermute x4, starting transfers between devices, ring(): return lax.ppermute(value, axis, pairs)  7.45 us
    pallas_call x5, Pallas kernels, run(): pl.pallas_call(kernel, out_shape=[jax.ShapeDtypeStruct(s, d) for s, d in...  6.17 us
    ppermute x4, waiting for transfers between devices, ring(): return lax.ppermute(value, axis, pairs)  2.84 us
  transfers between devices with their start and end apart: 5, of which 2 were waited for; matrix products, arithmetic and copies ran while one was open for 0% of the time, Pallas kernels for 5%

profile of v3, /device:TPU:1, one launch (start us, length us, event | category | flops | bytes accessed | tf_op | source)
XLA Modules:
  0.0 47.5 jit_solution(10298312159771152246)
XLA Ops:
  0.6 1.6 %shard_map.103 = (f32[19,8,8,128]{3,2,1,0:T(8,128)S(1)}, s32[64,128]{1,0:T(8,128)S(1)}, s32[2,1024]{1,0:T(2,128)S(1)}, f32[3,512]{1,0:T(4,128)S(1)}, f32[3,512]{...) custom-call(f32[19,8,8,128]{3,2,1,0:T(8,128)} %pop_in.1, ...), custom_call_target="tpu_custom_call" | custom-call | flops 1000000 | bytes 1048576 | tf_op jit(solution)/shard_map/pallas_call | solution.py:61
  2.2 11.5 %all-to-all-start = ((s32[128,1,128]{2,1,0:T(1,128)}), s32[128,1,128]{2,1,0:T(1,128)S(1)}, u32[]{:S(2)}, u32[]{:S(2)}) async-start(s32[128,1,128]{2,1,0:T(1,128)} %bitcast.4), calls=%async_computation | async-start | bytes 131072 | tf_op jit(solution)/shard_map/all_to_all | solution.py:552
  13.7 1.4 %collective-permute-start = (f32[56,128]{1,0:T(8,128)S(1)}, f32[56,128]{1,0:T(8,128)S(1)}, u32[]{:S(2)}, u32[]{:S(2)}) collective-permute-start(f32[56,128]{1,0:T(8,128)S(1)} %get-tuple-element.38), channel_id=1, source_target_pairs={{0,8},{8,16},{16,24},{24,32},{32,40},{40,48},{48,56},{56,64},{64,7... | collective-permute-start | bytes 86024 | tf_op jit(solution)/shard_map/ppermute | solution.py:548
  15.1 4.1 %collective-permute-start.1 = (f32[56,128]{1,0:T(8,128)S(1)}, f32[56,128]{1,0:T(8,128)S(1)}, u32[]{:S(2)}, u32[]{:S(2)}) collective-permute-start(f32[56,128]{1,0:T(8,128)S(1)} %get-tuple-element.39), channel_id=1, source_target_pairs={{8,0},{16,8},{24,16},{32,24},{40,32},{48,40},{56,48},{64,56},{72,6... | collective-permute-start | bytes 86024 | tf_op jit(solution)/shard_map/ppermute | solution.py:548
  19.2 1.8 %collective-permute-done.low = f32[56,128]{1,0:T(8,128)S(1)} collective-permute-done((f32[56,128]{1,0:T(8,128)S(1)}, f32[56,128]{1,0:T(8,128)S(1)}, u32[]{:S(2)}, u32[]{:S(2)}) %collective-permute-start) | collective-permute-done | bytes 28704 | tf_op jit(solution)/shard_map/ppermute | solution.py:548
  21.0 0.0 collective-permute-done.1.high
  21.1 1.9 %collective-permute-start.2 = (f32[64,128]{1,0:T(8,128)S(1)}, f32[64,128]{1,0:T(8,128)S(1)}, u32[]{:S(2)}, u32[]{:S(2)}) collective-permute-start(f32[64,128]{1,0:T(8,128)S(1)} %get-tuple-element.44), channel_id=1, source_target_pairs={{0,1},{1,2},{2,3},{3,4},{4,5},{5,6},{6,7},{7,0},{8,9},{9,10},{10,1... | collective-permute-start | bytes 98312 | tf_op jit(solution)/shard_map/ppermute | solution.py:548
  23.0 0.0 collective-permute-start.3
  23.0 2.3 %shard_map.104 = (f32[1216,128]{1,0:T(8,128)S(1)}, f32[72,128]{1,0:T(8,128)S(1)}, bf16[128,2048]{1,0:T(8,128)(2,1)S(1)}, bf16[128,1024]{1,0:T(8,128)(2,1)S(1)}, f32[56,128]{1,0:T(8,128)S(1)}) custom-call(f32[1216,128]{1,0:T(8,128)S(1)} %get-tuple-element.34.g, f32[64,128]{1,0:T(8,128)S(1)} %get-tuple-element.35.r, f32[1216,128]{1,0:T(8,128)S(1)} %bitcast.11, ...), custom_call_target="tpu_custom_call" | custom-call | flops 1000000 | bytes 1048576 | tf_op jit(solution)/shard_map/pallas_call | solution.py:61
  25.3 0.0 collective-permute-done.2.y_low
  25.3 1.0 %collective-permute-done.3.y_high = f32[64,128]{1,0:T(8,128)S(1)} collective-permute-done((f32[64,128]{1,0:T(8,128)S(1)}, f32[64,128]{1,0:T(8,128)S(1)}, u32[]{:S(2)}, u32[]{:S(2)}) %collective-permute-start.3) | collective-permute-done | bytes 32800 | tf_op jit(solution)/shard_map/ppermute | solution.py:548
  26.3 0.0 all-to-all-done
  26.3 0.6 %shard_map.106 = (f32[256,128]{1,0:T(8,128)S(1)}, s32[8,128]{1,0:T(8,128)S(1)}, f32[1216,128]{1,0:T(8,128)S(1)}) custom-call(s32[128,128]{1,0:T(8,128)S(1)} %bitcast.13, f32[3,512]{1,0:T(4,128)S(1)} %get-tuple-element.31.pos, f32[3,512]{1,0:T(4,128)S(1)} %get-tuple-element.32.vel, ...), custom_call_target="tpu_custom_call", output_to_operand_aliasing={{2}: (9, {})} | custom-call | flops 1000000 | bytes 1048576 | tf_op jit(solution)/shard_map/pallas_call | solution.py:61
  26.9 18.8 %all_to_all.16 = f32[128,2,128]{2,1,0:T(2,128)S(1)} all-to-all(f32[128,2,128]{2,1,0:T(2,128)S(1)} %bitcast.14), channel_id=1, replica_groups=mesh['gx'=16,'yz'=8] {'gx','yz'}, dimensions={0} | all-to-all | bytes 262144 | tf_op jit(solution)/shard_map/all_to_all | solution.py:552
  45.7 1.7 %shard_map.107 = (f32[1216,128]{1,0:T(8,128)}, f32[3,512]{1,0:T(4,128)}, f32[3,512]{1,0:T(4,128)}) custom-call(f32[256,128]{1,0:T(8,128)S(1)} %bitcast.12, s32[8,128]{1,0:T(8,128)S(1)} %get-tuple-element.49.rows_t, f32[1216,128]{1,0:T(8,128)S(1)} %get-tuple-element.50.base, f32[64,128]{1,0:T(8,128)S(1)} %get-tuple-element.35.r, ...), custom_call_target="tpu_custom_call" | custom-call | flops 1000000 | bytes 1048576 | tf_op jit(solution)/shard_map/pallas_call | solution.py:61
  (1 shorter events, 0.0 us)
Async XLA Ops:
  2.2 24.1 %all-to-all-start = ((s32[128,1,128]{2,1,0:T(1,128)}), s32[128,1,128]{2,1,0:T(1,128)S(1)}, u32[]{:S(2)}, u32[]{:S(2)}) async-start(s32[128,1,128]{2,1,0:T(1,128)} %bitcast.4), calls=%async_computation | async-start | bytes 131072 | tf_op jit(solution)/shard_map/all_to_all | solution.py:552
  13.7 7.3 %collective-permute-start = (f32[56,128]{1,0:T(8,128)S(1)}, f32[56,128]{1,0:T(8,128)S(1)}, u32[]{:S(2)}, u32[]{:S(2)}) collective-permute-start(f32[56,128]{1,0:T(8,128)S(1)} %get-tuple-element.38), channel_id=1, source_target_pairs={{0,8},{8,16},{16,24},{24,32},{32,40},{40,48},{48,56},{56,64},{64,7... | collective-permute-start | bytes 86024 | tf_op jit(solution)/shard_map/ppermute | solution.py:548
  15.1 5.9 %collective-permute-start.1 = (f32[56,128]{1,0:T(8,128)S(1)}, f32[56,128]{1,0:T(8,128)S(1)}, u32[]{:S(2)}, u32[]{:S(2)}) collective-permute-start(f32[56,128]{1,0:T(8,128)S(1)} %get-tuple-element.39), channel_id=1, source_target_pairs={{8,0},{16,8},{24,16},{32,24},{40,32},{48,40},{56,48},{64,56},{72,6... | collective-permute-start | bytes 86024 | tf_op jit(solution)/shard_map/ppermute | solution.py:548
  21.1 4.2 %collective-permute-start.2 = (f32[64,128]{1,0:T(8,128)S(1)}, f32[64,128]{1,0:T(8,128)S(1)}, u32[]{:S(2)}, u32[]{:S(2)}) collective-permute-start(f32[64,128]{1,0:T(8,128)S(1)} %get-tuple-element.44), channel_id=1, source_target_pairs={{0,1},{1,2},{2,3},{3,4},{4,5},{5,6},{6,7},{7,0},{8,9},{9,10},{10,1... | collective-permute-start | bytes 98312 | tf_op jit(solution)/shard_map/ppermute | solution.py:548
  23.0 3.3 %collective-permute-start.3 = (f32[64,128]{1,0:T(8,128)S(1)}, f32[64,128]{1,0:T(8,128)S(1)}, u32[]{:S(2)}, u32[]{:S(2)}) collective-permute-start(f32[64,128]{1,0:T(8,128)S(1)} %get-tuple-element.45), channel_id=1, source_target_pairs={{1,0},{2,1},{3,2},{4,3},{5,4},{6,5},{7,6},{0,7},{9,8},{10,9},{11,1... | collective-permute-start | bytes 98312 | tf_op jit(solution)/shard_map/ppermute | solution.py:548

commit v4 on v3

--- a/solution.py
+++ b/solution.py
@@ -36,7 +36,7 @@
 from_low_x = (1, 7, 9, 11, 13)
 from_high_x = (2, 8, 10, 12, 14)
 from_low_y = (3, 7, 10, 15, 17)
-from_high_y = (4, 8, 9, 16, 18)
+from_high_y = (4, 9, 8, 18, 16)
 
 fields = ((1, 0, 0), (0, 1, 0), (0, 0, 1), (1, 1, 0), (1, -1, 0), (1, 0, 1), (1, 0, -1), (0, 1, 1), (0, 1, -1))
 
@@ -190,7 +190,7 @@
     sent.wait()
 
 
-def corner_kernel(y_up, y_down, low, high, out_up, out_down):
+def corner_kernel(y_up, y_down, low, high, out_one, out_two, out_up, out_down):
     zero = jnp.zeros((2, 128), f32)
     for src, out, y, k_low, k_high in (
         (y_up, out_up, WY - 1, from_low_x.index(7), from_high_x.index(10)),
@@ -202,6 +202,9 @@
             out[at + 1 : at + 2, :] = halo[40 + y : 41 + y, :]
             out[at + 2 : at + 3, :] = halo[48 + y : 49 + y, :]
         out[62:64, :] = zero
+    even = lax.rem(lax.axis_index("yz"), 2) == 0
+    out_one[...] = jnp.where(even, out_up[...], out_down[...])
+    out_two[...] = jnp.where(even, out_down[...], out_up[...])
 
 
 def shift_y(value, c_y, row):
@@ -254,21 +257,18 @@
     return low[40:48, :] if at == -1 else high[40:48, :] if at == WX else r[at * 8 : at * 8 + 8, :]
 
 
-def spread_slots(part, row, pick):
-    halves = []
-    for half in range(2):
-        rows_v = [
-            jnp.where(pick, spread(part[half * 72 + v * 8 + row : half * 72 + v * 8 + row + 1, :]), 0.0) for v in range(9)
-        ]
-        halves.append(jnp.concatenate(rows_v + [jnp.zeros((8, 128), f32)], 0).astype(jnp.bfloat16))
-    return jnp.concatenate(halves, 0)
+def spread_slots(part, row, pick, names=range(9)):
+    tiles = [
+        jnp.where(pick, spread(part[half * 72 + v * 8 + row : half * 72 + v * 8 + row + 1, :]), 0.0)
+        for half in range(2)
+        for v in names
+    ]
+    return jnp.concatenate(tiles, 0).astype(jnp.bfloat16)
 
 
 def split_fields(part, acc):
     for v in range(9):
         if acc[v] is None:
-            part[v * 8 : v * 8 + 8, :] = jnp.zeros((8, 128), f32)
-            part[72 + v * 8 : 80 + v * 8, :] = jnp.zeros((8, 128), f32)
             continue
         value = 2.0 * acc[v] if v < 3 else acc[v]
         head = value.astype(jnp.bfloat16).astype(f32)
@@ -300,7 +300,7 @@
             if 0 <= at < WX or c_y == 0 or c_z == 0:
                 shifted[k * 80 + (at + 1) * 8 : k * 80 + (at + 1) * 8 + 8, :] = shift(plain, c_y, c_z)
     number = lax.broadcasted_iota(i32, (128, 128), 0)
-    total = jnp.zeros((160, 128), f32)
+    total = jnp.zeros((144, 128), f32)
     for x in range(WX):
         fluid = ids[x * 8 : x * 8 + 8, :] < 0
         base[x * 8 : x * 8 + 8, :] = jnp.where(fluid, g[x * 8 : x * 8 + 8, :], pop[x * 8 : x * 8 + 8, :])
@@ -326,7 +326,7 @@
                 to = (0 if y == 0 else 1024) + x * 128
                 edge_hot[:, to : to + 128] = one_hot
         total = total + contract(left[...], hot[...])
-    sums[...] = total[0:72, :] + total[80:152, :]
+    sums[...] = total[0:72, :] + total[72:144, :]
     for k in range(8):
         key = pairs[0:1, k * 128 : k * 128 + 128]
         pair[k : k + 1, :] = key
@@ -338,33 +338,40 @@
         state[c * 8 : c * 8 + 8, :] = value
 
 
-def complete_rows(ids, y_low, y_high, edge_hot, base, part, left):
+edge_fields = (0, 1, 2, 3, 4, 5, 6, 8)
+
+
+def complete_side(low_side, ids, halo, edge_hot, base, part, left):
     sub = sublane_iota()
-    total = jnp.zeros((160, 128), f32)
-    for side, (y, halo, names) in enumerate(((0, y_low, from_low_y), (WY - 1, y_high, from_high_y))):
-        fluid = ids[pl.ds(y, 8, stride=8), :] < 0
-        links = Totals()
-        for k, direction in enumerate(names):
-            c_x, _, c_z = lattice_dirs[direction]
-            came = halo[k * 8 : k * 8 + 8, :]
-            near_r = halo[40:48, :]
-            if c_x == 1:
-                came = jnp.where(sub == 0, spread(halo[56:57, :]), pltpu.roll(came, 1, 0))
-                near_r = jnp.where(sub == 0, spread(halo[57:58, :]), pltpu.roll(near_r, 1, 0))
-            elif c_x == -1:
-                came = jnp.where(sub == WX - 1, spread(halo[59:60, :]), pltpu.roll(came, WX - 1, 0))
-                near_r = jnp.where(sub == WX - 1, spread(halo[60:61, :]), pltpu.roll(near_r, WX - 1, 0))
-            came = shift_z(came, c_z)
-            near_r = shift_z(near_r, c_z)
-            at = pl.ds(direction * ROWS + y, 8, stride=8)
-            base[at, :] = jnp.where(fluid & (near_r != 0.0), came, base[at, :])
-            links.link(direction, came, near_r)
-        split_fields(part, links.acc)
-        for x in range(WX):
-            key = ids[x * 8 + y : x * 8 + y + 1, :]
-            left[:, x * 128 : x * 128 + 128] = spread_slots(part, x, spread(key & 7) == sub)
-        total = total + contract(left[...], edge_hot[:, side * 1024 : side * 1024 + 1024])
-    return total[0:72, :] + total[80:152, :]
+    y = jnp.where(low_side, 0, WY - 1)
+    sign = jnp.where(low_side, 1.0, -1.0)
+    fluid = ids[pl.ds(y, 8, stride=8), :] < 0
+    links = Totals()
+    for k, direction in enumerate(from_low_y):
+        c_x, _, c_z = lattice_dirs[direction]
+        came = halo[k * 8 : k * 8 + 8, :]
+        near_r = halo[40:48, :]
+        if c_x == 1:
+            came = jnp.where(sub == 0, spread(halo[56:57, :]), pltpu.roll(came, 1, 0))
+            near_r = jnp.where(sub == 0, spread(halo[57:58, :]), pltpu.roll(near_r, 1, 0))
+        elif c_x == -1:
+            came = jnp.where(sub == WX - 1, spread(halo[59:60, :]), pltpu.roll(came, WX - 1, 0))
+            near_r = jnp.where(sub == WX - 1, spread(halo[60:61, :]), pltpu.roll(near_r, WX - 1, 0))
+        came = shift_z(came, c_z)
+        near_r = shift_z(near_r, c_z)
+        at = pl.ds(jnp.where(low_side, direction, from_high_y[k]) * ROWS + y, 8, stride=8)
+        base[at, :] = jnp.where(fluid & (near_r != 0.0), came, base[at, :])
+        links.link(direction, came, near_r)
+    for v in (1, 6, 8):
+        links.acc[v] = sign * links.acc[v]
+    split_fields(part, links.acc)
+    for x in range(WX):
+        key = ids[pl.ds(x * 8 + y, 1), :]
+        left[:, x * 128 : x * 128 + 128] = spread_slots(part, x, spread(key & 7) == sub, edge_fields)
+    hot = edge_hot[:, pl.ds(pl.multiple_of(jnp.where(low_side, 0, 1024), 1024), 1024)]
+    total = contract(left[...], hot)
+    total = total[0:64, :] + total[64:128, :]
+    return jnp.concatenate([total[0:56, :], jnp.zeros((8, 128), f32), total[56:64, :]], 0)
 
 
 def held_states(pos, vel, rad, chunk, index):
@@ -380,9 +387,12 @@
 
 
 def reply_kernel(
-    got, pos, vel, rad, sums, ids, y_low, y_high, edge_hot, base_in, out, rows_t, base, part, left
+    got, pos, vel, rad, sums_in, ids, y_one, y_two, edge_hot, base_in, out, rows_t, base, y_low, y_high, part, left
 ):
-    sums = sums[...] + complete_rows(ids, y_low, y_high, edge_hot, base, part, left)
+    even = lax.rem(lax.axis_index("yz"), 2) == 0
+    sums = sums_in[...] + complete_side(even, ids, y_two, edge_hot, base, part, left)
+    y_low[...] = jnp.where(even, y_two[...], y_one[...])
+    y_high[...] = jnp.where(even, y_one[...], y_two[...])
     rows = got[...].astype(f32).T[0:8, :].astype(i32)
     rows_t[...] = rows
     state = held_states(pos, vel, rad, rows >> 7, rows & 127)
@@ -401,9 +411,14 @@
     rest = []
     for d_x, d_y in ((-1, 0), (1, 0), (0, -1), (0, 1)):
         rest += [moved(value, d_x, d_y) for value in speed]
-    for d_x, d_y, value in ((-1, -1, plus), (-1, 1, minus), (1, -1, minus), (1, 1, plus)):
+    for d_x, d_y, value in ((-1, -1, plus), (1, -1, minus), (-1, 1, minus), (1, 1, plus)):
         rest.append(moved(value, d_x, d_y))
     out[pl.ds(1, 128, stride=2), :] = jnp.concatenate(rest, 0).T
+
+
+def half_kernel(sums_in, ids, y_one, edge_hot, base_in, base, sums, part, left):
+    low_side = lax.rem(lax.axis_index("yz"), 2) == 1
+    sums[...] = sums_in[...] + complete_side(low_side, ids, y_one, edge_hot, base, part, left)
 
 
 def look_up(ref, starts, cell):
@@ -425,6 +440,11 @@
 ):
     table[...] = got[pl.ds(0, 128, stride=2), :].T
     around[...] = got[pl.ds(1, 128, stride=2), :].T
+    number = lax.broadcasted_iota(i32, (128, 128), 0)
+    for s in range(8):
+        key = rows_t[s : s + 1, :]
+        below = jnp.broadcast_to(jnp.where(key >= 0, key & 127, -1), (128, 128))
+        hot[:, s * 128 : s * 128 + 128] = jnp.where(below == number, 1.0, 0.0).astype(jnp.bfloat16)
 
     def combine(values, vector):
         total = None
@@ -444,14 +464,20 @@
         for n, vector in enumerate(fields):
             if vector[0] != 0:
                 moving[n * 80 + (at + 1) * 8 : n * 80 + (at + 1) * 8 + 8, :] = combine(speeds, vector)
-    for side, halo, start, first, second in ((0, y_low, 48, 96, 112), (1, y_high, 72, 104, 120)):
+    for side, halo, start in ((0, y_low, 48), (1, y_high, 72)):
         speeds = look_up(around, (start, start + 8, start + 16), halo[48:56, :].astype(i32))
         for n, vector in enumerate(fields):
             if vector[1] != 0:
-                rim[side * 88 + n * 8 : side * 88 + n * 8 + 8, :] = combine(speeds, vector)
-        for n, (row, start_row) in enumerate(((58, first), (61, second))):
-            (value,) = look_up(around, (start_row,), spread(halo[row : row + 1, :]).astype(i32))
-            rim[side * 88 + 72 + n * 8 : side * 88 + 80 + n * 8, :] = value
+                rim[side * 72 + n * 8 : side * 72 + n * 8 + 8, :] = combine(speeds, vector)
+    for n, (halo, row) in enumerate(((y_low, 58), (y_low, 61), (y_high, 58), (y_high, 61))):
+        pair[n : n + 1, :] = halo[row : row + 1, :].astype(i32)
+    cell = pair[0:4, :]
+    owner = (cell >> 3) & 127
+    slot = jnp.where(cell >= 0, cell & 7, 8)
+    value = jnp.zeros((4, 128), f32)
+    for s in range(8):
+        value = jnp.where(slot == s, lane_take(around[pl.ds(96 + s, 4, stride=8), :], owner), value)
+    rim[144:148, :] = value
 
     for x in range(WX):
         mine = r[x * 8 : x * 8 + 8, :]
@@ -463,7 +489,7 @@
             value = moving[n * 80 + (at + 1) * 8 : n * 80 + (at + 1) * 8 + 8, :]
             if c_y != 0:
                 side = 0 if c_y == 1 else 1
-                row = side * 88 + (72 if at == -1 else 80 if at == WX else n * 8 + at)
+                row = 144 + side * 2 if at == -1 else 145 + side * 2 if at == WX else side * 72 + n * 8 + at
                 value = shift_y(value, c_y, rim[row : row + 1, :])
             value = shift_z(value, c_z)
             to = direction * ROWS + x * 8
@@ -502,7 +528,6 @@
     push = [size * n for n in normal]
 
     sub = sublane_iota()
-    number = lax.broadcasted_iota(i32, (128, 128), 0)
 
     def by_block(values, key):
         pick = spread(key >> 7) == (sub & 3)
@@ -521,8 +546,6 @@
         columns = slice(s * 128, s * 128 + 128)
         key = rows_t[s : s + 1, :]
         left[0:80, columns] = by_block([table[56 + v * 8 + s : 57 + v * 8 + s, :] for v in range(9)], key)
-        rest = jnp.broadcast_to(jnp.where(key >= 0, key & 127, -1), (128, 128))
-        hot[:, columns] = jnp.where(rest == number, 1.0, 0.0).astype(jnp.bfloat16)
         left[80:112, columns] = by_block([p[s : s + 1, :] for p in push], pairs[0:1, columns])
     fluid = contract(left[0:80, :], hot[...])
     fluid = fluid[0:40, :] + fluid[40:80, :]
@@ -545,6 +568,14 @@
 def ring(axis, value, up):
     count = lax.axis_size(axis)
     pairs = [(i, (i + 1) % count) if up else ((i + 1) % count, i) for i in range(count)]
+    return lax.ppermute(value, axis, pairs)
+
+
+def swap(axis, value, offset):
+    count = lax.axis_size(axis)
+    pairs = []
+    for i in range(offset, count + offset, 2):
+        pairs += [(i % count, (i + 1) % count), ((i + 1) % count, i % count)]
     return lax.ppermute(value, axis, pairs)
 
 
@@ -593,26 +624,32 @@
     low = ring("gx", x_up, True)
     high = ring("gx", x_down, False)
     asked = exchange(ask)
-    y_up, y_down = call(corner_kernel, [((64, 128), f32), ((64, 128), f32)])(y_up, y_down, low, high)
-    y_low = ring("yz", y_up, True)
-    y_high = ring("yz", y_down, False)
+    y_one, y_two = call(
+        corner_kernel, [((64, 128), f32), ((64, 128), f32)], [pltpu.VMEM((64, 128), f32)] * 2
+    )(y_up, y_down, low, high)
+    y_one = swap("yz", y_one, 0)
+    y_two = swap("yz", y_two, 1)
     base, sums, edge_hot, pair_hot, state = call(
         early_kernel,
         [full, ((72, 128), f32), ((128, 2048), bf16), ((128, 1024), bf16), ((56, 128), f32)],
         [
             pltpu.VMEM((9 * 80, 128), f32),
             pltpu.VMEM((144, 128), f32),
-            pltpu.VMEM((160, 1024), bf16),
+            pltpu.VMEM((144, 1024), bf16),
             pltpu.VMEM((128, 1024), bf16),
             pltpu.VMEM((8, 128), i32),
         ],
     )(g, r, pop, ids, low, high, pairs, pos, vel, rad)
-    send, rows_t, base = call(
+    tail = [pltpu.VMEM((144, 128), f32), pltpu.VMEM((128, 1024), bf16)]
+    base, sums = call(half_kernel, [full, ((72, 128), f32)], tail, aliases={4: 0})(
+        sums, ids, y_one, edge_hot, base
+    )
+    send, rows_t, base, y_low, y_high = call(
         reply_kernel,
-        [((256, 128), f32), ((8, 128), i32), full],
-        [pltpu.VMEM((144, 128), f32), pltpu.VMEM((160, 1024), bf16)],
+        [((256, 128), f32), ((8, 128), i32), full, ((64, 128), f32), ((64, 128), f32)],
+        tail,
         aliases={9: 2},
-    )(asked, pos, vel, rad, sums, ids, y_low, y_high, edge_hot, base)
+    )(asked, pos, vel, rad, sums, ids, y_one, y_two, edge_hot, base)
     got = exchange(send.reshape(128, 2, 128)).reshape(256, 128)
     read, vel_next, pos_next = call(
         last_kernel,
@@ -624,7 +661,7 @@
             pltpu.VMEM((128, 128), f32),
             pltpu.VMEM((128, 128), f32),
             pltpu.VMEM((9 * 80, 128), f32),
-            pltpu.VMEM((2 * 88, 128), f32),
+            pltpu.VMEM((152, 128), f32),
             pltpu.VMEM((112, 1024), bf16),
             pltpu.VMEM((128, 1024), bf16),
             pltpu.VMEM((8, 128), i32),

time: 47.7 us -> 47.5 us (level)
  waiting for transfers between devices: 2.84 us -> 1.82 us
  blocking collectives: 18.8 us -> 19.4 us
    ppermute x0 -> x2, starting transfers between devices: none -> 2.06 us  [swap(): return lax.ppermute(value, axis, pairs)]
    ppermute x4 -> x2, starting transfers between devices: 7.45 us -> 5.54 us  [ring(): return lax.ppermute(value, axis, pairs)]
    ppermute x4 -> x2, waiting for transfers between devices: 2.84 us -> 1.81 us  [ring(): return lax.ppermute(value, axis, pairs)]
    all_to_all x1, blocking collectives: 18.8 us -> 19.4 us  [exchange(): lax.all_to_all(value, ('gx', 'yz'), split_axis=0, concat_axis=0, tiled=True)]
    pallas_call x5 -> x6, Pallas kernels: 6.17 us -> 6.3 us  [run(): pl.pallas_call(kernel, out_shape=[jax.ShapeDtypeStruct(s, d) for s, d in...]
  transfers between devices with their start and end apart: 5 -> 5, of which waited for: 2 -> 1; matrix products, arithmetic and copies ran while one was open for 0% -> 0% of each run, Pallas kernels for 5% -> 5%
where the time goes in v4:
time: 47.5 us; the launch traced here: 47.3 us
  blocking collectives  19.4 us (41%)
  starting transfers between devices  19.1 us (40%)
  Pallas kernels  6.3 us (13%)
  waiting for transfers between devices  1.82 us (4%)
  between operations  0.69 us (1%)
    all_to_all x1, blocking collectives, exchange(): lax.all_to_all(value, ('gx', 'yz'), split_axis=0, concat_axis=0, tiled=True)  19.4 us
    all_to_all x1, starting transfers between devices, exchange(): lax.all_to_all(value, ('gx', 'yz'), split_axis=0, concat_axis=0, tiled=True)  11.5 us
    pallas_call x6, Pallas kernels, run(): pl.pallas_call(kernel, out_shape=[jax.ShapeDtypeStruct(s, d) for s, d in...  6.3 us
    ppermute x2, starting transfers between devices, ring(): return lax.ppermute(value, axis, pairs)  5.54 us
    ppermute x2, starting transfers between devices, swap(): return lax.ppermute(value, axis, pairs)  2.06 us
    ppermute x2, waiting for transfers between devices, ring(): return lax.ppermute(value, axis, pairs)  1.81 us
  transfers between devices with their start and end apart: 5, of which 1 were waited for; matrix products, arithmetic and copies ran while one was open for 0% of the time, Pallas kernels for 5%

profile of v4, /device:TPU:1, one launch (start us, length us, event | category | flops | bytes accessed | tf_op | source)
XLA Modules:
  0.0 47.3 jit_solution(10888404837219077802)
XLA Ops:
  0.6 1.6 %shard_map.103 = (f32[19,8,8,128]{3,2,1,0:T(8,128)S(1)}, s32[64,128]{1,0:T(8,128)S(1)}, s32[2,1024]{1,0:T(2,128)S(1)}, f32[3,512]{1,0:T(4,128)S(1)}, f32[3,512]{...) custom-call(f32[19,8,8,128]{3,2,1,0:T(8,128)} %pop_in.1, ...), custom_call_target="tpu_custom_call" | custom-call | flops 1000000 | bytes 1048576 | tf_op jit(solution)/shard_map/pallas_call | solution.py:61
  2.2 11.5 %all-to-all-start = ((s32[128,1,128]{2,1,0:T(1,128)}), s32[128,1,128]{2,1,0:T(1,128)S(1)}, u32[]{:S(2)}, u32[]{:S(2)}) async-start(s32[128,1,128]{2,1,0:T(1,128)} %bitcast.4), calls=%async_computation | async-start | bytes 131072 | tf_op jit(solution)/shard_map/all_to_all | solution.py:583
  13.7 1.4 %collective-permute-start = (f32[56,128]{1,0:T(8,128)S(1)}, f32[56,128]{1,0:T(8,128)S(1)}, u32[]{:S(2)}, u32[]{:S(2)}) collective-permute-start(f32[56,128]{1,0:T(8,128)S(1)} %get-tuple-element.42), channel_id=1, source_target_pairs={{0,8},{8,16},{16,24},{24,32},{32,40},{40,48},{48,56},{56,64},{64,7... | collective-permute-start | bytes 86024 | tf_op jit(solution)/shard_map/ppermute | solution.py:571
  15.1 4.1 %collective-permute-start.1 = (f32[56,128]{1,0:T(8,128)S(1)}, f32[56,128]{1,0:T(8,128)S(1)}, u32[]{:S(2)}, u32[]{:S(2)}) collective-permute-start(f32[56,128]{1,0:T(8,128)S(1)} %get-tuple-element.43), channel_id=1, source_target_pairs={{8,0},{16,8},{24,16},{32,24},{40,32},{48,40},{56,48},{64,56},{72,6... | collective-permute-start | bytes 86024 | tf_op jit(solution)/shard_map/ppermute | solution.py:571
  19.2 1.8 %collective-permute-done.low = f32[56,128]{1,0:T(8,128)S(1)} collective-permute-done((f32[56,128]{1,0:T(8,128)S(1)}, f32[56,128]{1,0:T(8,128)S(1)}, u32[]{:S(2)}, u32[]{:S(2)}) %collective-permute-start) | collective-permute-done | bytes 28704 | tf_op jit(solution)/shard_map/ppermute | solution.py:571
  21.0 0.0 collective-permute-done.1.high
  21.1 1.1 %collective-permute-start.2 = (f32[64,128]{1,0:T(8,128)S(1)}, f32[64,128]{1,0:T(8,128)S(1)}, u32[]{:S(2)}, u32[]{:S(2)}) collective-permute-start(f32[64,128]{1,0:T(8,128)S(1)} %get-tuple-element.48), channel_id=1, source_target_pairs={{0,1},{1,0},{2,3},{3,2},{4,5},{5,4},{6,7},{7,6},{8,9},{9,8},{10,11... | collective-permute-start | bytes 98312 | tf_op jit(solution)/shard_map/ppermute | solution.py:579
  22.2 1.0 %collective-permute-start.3 = (f32[64,128]{1,0:T(8,128)S(1)}, f32[64,128]{1,0:T(8,128)S(1)}, u32[]{:S(2)}, u32[]{:S(2)}) collective-permute-start(f32[64,128]{1,0:T(8,128)S(1)} %get-tuple-element.52), channel_id=1, source_target_pairs={{1,2},{2,1},{3,4},{4,3},{5,6},{6,5},{7,0},{0,7},{9,10},{10,9},{11,... | collective-permute-start | bytes 98312 | tf_op jit(solution)/shard_map/ppermute | solution.py:579
  23.1 2.2 %shard_map.104 = (f32[1216,128]{1,0:T(8,128)S(1)}, f32[72,128]{1,0:T(8,128)S(1)}, bf16[128,2048]{1,0:T(8,128)(2,1)S(1)}, bf16[128,1024]{1,0:T(8,128)(2,1)S(1)}, f32[56,128]{1,0:T(8,128)S(1)}) custom-call(f32[1216,128]{1,0:T(8,128)S(1)} %get-tuple-element.38.g, f32[64,128]{1,0:T(8,128)S(1)} %get-tuple-element.39.r, f32[1216,128]{1,0:T(8,128)S(1)} %bitcast.11, ...), custom_call_target="tpu_custom_call" | custom-call | flops 1000000 | bytes 1048576 | tf_op jit(solution)/shard_map/pallas_call | solution.py:61
  25.4 0.0 collective-permute-done.2.y_one
  25.4 0.3 shard_map.106
  25.7 0.0 collective-permute-done.3.y_two
  25.7 0.0 all-to-all-done
  25.7 0.4 shard_map.107
  26.2 19.4 %all_to_all.16 = f32[128,2,128]{2,1,0:T(2,128)S(1)} all-to-all(f32[128,2,128]{2,1,0:T(2,128)S(1)} %bitcast.14), channel_id=1, replica_groups=mesh['gx'=16,'yz'=8] {'gx','yz'}, dimensions={0} | all-to-all | bytes 262144 | tf_op jit(solution)/shard_map/all_to_all | solution.py:583
  45.6 1.7 %shard_map.108 = (f32[1216,128]{1,0:T(8,128)}, f32[3,512]{1,0:T(4,128)}, f32[3,512]{1,0:T(4,128)}) custom-call(f32[256,128]{1,0:T(8,128)S(1)} %bitcast.12, s32[8,128]{1,0:T(8,128)S(1)} %get-tuple-element.55.rows_t, f32[1216,128]{1,0:T(8,128)S(1)} %get-tuple-element.56.base, f32[64,128]{1,0:T(8,128)S(1)} %get-tuple-element.39.r, ...), custom_call_target="tpu_custom_call" | custom-call | flops 1000000 | bytes 1048576 | tf_op jit(solution)/shard_map/pallas_call | solution.py:61
  (1 shorter events, 0.0 us)
Async XLA Ops:
  2.2 23.5 %all-to-all-start = ((s32[128,1,128]{2,1,0:T(1,128)}), s32[128,1,128]{2,1,0:T(1,128)S(1)}, u32[]{:S(2)}, u32[]{:S(2)}) async-start(s32[128,1,128]{2,1,0:T(1,128)} %bitcast.4), calls=%async_computation | async-start | bytes 131072 | tf_op jit(solution)/shard_map/all_to_all | solution.py:583
  13.7 7.3 %collective-permute-start = (f32[56,128]{1,0:T(8,128)S(1)}, f32[56,128]{1,0:T(8,128)S(1)}, u32[]{:S(2)}, u32[]{:S(2)}) collective-permute-start(f32[56,128]{1,0:T(8,128)S(1)} %get-tuple-element.42), channel_id=1, source_target_pairs={{0,8},{8,16},{16,24},{24,32},{32,40},{40,48},{48,56},{56,64},{64,7... | collective-permute-start | bytes 86024 | tf_op jit(solution)/shard_map/ppermute | solution.py:571
  15.1 5.9 %collective-permute-start.1 = (f32[56,128]{1,0:T(8,128)S(1)}, f32[56,128]{1,0:T(8,128)S(1)}, u32[]{:S(2)}, u32[]{:S(2)}) collective-permute-start(f32[56,128]{1,0:T(8,128)S(1)} %get-tuple-element.43), channel_id=1, source_target_pairs={{8,0},{16,8},{24,16},{32,24},{40,32},{48,40},{56,48},{64,56},{72,6... | collective-permute-start | bytes 86024 | tf_op jit(solution)/shard_map/ppermute | solution.py:571
  21.1 4.3 %collective-permute-start.2 = (f32[64,128]{1,0:T(8,128)S(1)}, f32[64,128]{1,0:T(8,128)S(1)}, u32[]{:S(2)}, u32[]{:S(2)}) collective-permute-start(f32[64,128]{1,0:T(8,128)S(1)} %get-tuple-element.48), channel_id=1, source_target_pairs={{0,1},{1,0},{2,3},{3,2},{4,5},{5,4},{6,7},{7,6},{8,9},{9,8},{10,11... | collective-permute-start | bytes 98312 | tf_op jit(solution)/shard_map/ppermute | solution.py:579
  22.2 3.5 %collective-permute-start.3 = (f32[64,128]{1,0:T(8,128)S(1)}, f32[64,128]{1,0:T(8,128)S(1)}, u32[]{:S(2)}, u32[]{:S(2)}) collective-permute-start(f32[64,128]{1,0:T(8,128)S(1)} %get-tuple-element.52), channel_id=1, source_target_pairs={{1,2},{2,1},{3,4},{4,3},{5,6},{6,5},{7,0},{0,7},{9,10},{10,9},{11,... | collective-permute-start | bytes 98312 | tf_op jit(solution)/shard_map/ppermute | solution.py:579

commit v5 on v4

--- a/solution.py
+++ b/solution.py
@@ -146,12 +146,6 @@
         [copy(2 + 2 * n + m, pop_in.at[:, x], pop.at[:, x]) for m, x in enumerate(chunk)]
         for n, chunk in enumerate(planes)
     ]
-    others = [
-        copy(10 + k, src, dst)
-        for k, (src, dst) in enumerate(
-            ((pairs_in, pairs), (pos_in, pos), (vel_in, vel), (rad_in, rad), (mass_in, mass))
-        )
-    ]
     asking.wait()
     lane = lane_iota()
     sub = sublane_iota()
@@ -160,6 +154,12 @@
         index = (8 * (tile % 2) + sub) * 8 + (lane & 7)
         ask[tile * 8 : tile * 8 + 8, :] = lane_take(spread(row), index)
     sent = copy(15, ask, ask_out)
+    others = [
+        copy(10 + k, src, dst)
+        for k, (src, dst) in enumerate(
+            ((pairs_in, pairs), (pos_in, pos), (vel_in, vel), (rad_in, rad), (mass_in, mass))
+        )
+    ]
     cells.wait()
     for n, x in ((n, x) for n, chunk in enumerate(planes) for x in chunk):
         if x == planes[n][0]:
@@ -387,7 +387,7 @@
 
 
 def reply_kernel(
-    got, pos, vel, rad, sums_in, ids, y_one, y_two, edge_hot, base_in, out, rows_t, base, y_low, y_high, part, left
+    got, pos, vel, rad, sums_in, ids, y_one, y_two, edge_hot, base_in, out, rows_t, hot, base, y_low, y_high, part, left
 ):
     even = lax.rem(lax.axis_index("yz"), 2) == 0
     sums = sums_in[...] + complete_side(even, ids, y_two, edge_hot, base, part, left)
@@ -414,6 +414,11 @@
     for d_x, d_y, value in ((-1, -1, plus), (1, -1, minus), (-1, 1, minus), (1, 1, plus)):
         rest.append(moved(value, d_x, d_y))
     out[pl.ds(1, 128, stride=2), :] = jnp.concatenate(rest, 0).T
+    number = lax.broadcasted_iota(i32, (128, 128), 0)
+    for s in range(8):
+        key = rows[s : s + 1, :]
+        below = jnp.broadcast_to(jnp.where(key >= 0, key & 127, -1), (128, 128))
+        hot[:, s * 128 : s * 128 + 128] = jnp.where(below == number, 1.0, 0.0).astype(jnp.bfloat16)
 
 
 def half_kernel(sums_in, ids, y_one, edge_hot, base_in, base, sums, part, left):
@@ -434,17 +439,12 @@
 
 
 def last_kernel(
-    got, rows_t, base, r, ids, low, high, y_low, y_high, pairs, pair_hot, state, pos, vel, mass,
+    got, rows_t, hot, base, r, ids, low, high, y_low, y_high, pairs, pair_hot, state, pos, vel, mass,
     read_out, vel_out, pos_out,
-    read, vel_next, pos_next, table, around, moving, rim, left, hot, pair, sems,
+    read, vel_next, pos_next, table, around, moving, rim, left, pair, sems,
 ):
     table[...] = got[pl.ds(0, 128, stride=2), :].T
     around[...] = got[pl.ds(1, 128, stride=2), :].T
-    number = lax.broadcasted_iota(i32, (128, 128), 0)
-    for s in range(8):
-        key = rows_t[s : s + 1, :]
-        below = jnp.broadcast_to(jnp.where(key >= 0, key & 127, -1), (128, 128))
-        hot[:, s * 128 : s * 128 + 128] = jnp.where(below == number, 1.0, 0.0).astype(jnp.bfloat16)
 
     def combine(values, vector):
         total = None
@@ -644,11 +644,11 @@
     base, sums = call(half_kernel, [full, ((72, 128), f32)], tail, aliases={4: 0})(
         sums, ids, y_one, edge_hot, base
     )
-    send, rows_t, base, y_low, y_high = call(
+    send, rows_t, list_hot, base, y_low, y_high = call(
         reply_kernel,
-        [((256, 128), f32), ((8, 128), i32), full, ((64, 128), f32), ((64, 128), f32)],
+        [((256, 128), f32), ((8, 128), i32), ((128, 1024), bf16), full, ((64, 128), f32), ((64, 128), f32)],
         tail,
-        aliases={9: 2},
+        aliases={9: 3},
     )(asked, pos, vel, rad, sums, ids, y_one, y_two, edge_hot, base)
     got = exchange(send.reshape(128, 2, 128)).reshape(256, 128)
     read, vel_next, pos_next = call(
@@ -663,12 +663,11 @@
             pltpu.VMEM((9 * 80, 128), f32),
             pltpu.VMEM((152, 128), f32),
             pltpu.VMEM((112, 1024), bf16),
-            pltpu.VMEM((128, 1024), bf16),
             pltpu.VMEM((8, 128), i32),
             pltpu.SemaphoreType.DMA((3,)),
         ],
         out_specs=[HBM] * 3,
-    )(got, rows_t, base, r, ids, low, high, y_low, y_high, pairs, pair_hot, state, pos, vel, mass)
+    )(got, rows_t, list_hot, base, r, ids, low, high, y_low, y_high, pairs, pair_hot, state, pos, vel, mass)
     return (read.reshape(19, WX, WY, WZ), vel_next, pos_next)
 
 

time: 47.5 us -> 47.8 us (level)
  no operation moved by 1% of the time
where the time goes in v5:
time: 47.8 us; the launch traced here: 47.5 us
  blocking collectives  19.4 us (41%)
  starting transfers between devices  19.1 us (40%)
  Pallas kernels  6.49 us (14%)
  waiting for transfers between devices  1.82 us (4%)
  between operations  0.7 us (1%)
    all_to_all x1, blocking collectives, exchange(): lax.all_to_all(value, ('gx', 'yz'), split_axis=0, concat_axis=0, tiled=True)  19.4 us
    all_to_all x1, starting transfers between devices, exchange(): lax.all_to_all(value, ('gx', 'yz'), split_axis=0, concat_axis=0, tiled=True)  11.5 us
    pallas_call x6, Pallas kernels, run(): pl.pallas_call(kernel, out_shape=[jax.ShapeDtypeStruct(s, d) for s, d in...  6.49 us
    ppermute x2, starting transfers between devices, ring(): return lax.ppermute(value, axis, pairs)  5.54 us
    ppermute x2, starting transfers between devices, swap(): return lax.ppermute(value, axis, pairs)  2.06 us
    ppermute x2, waiting for transfers between devices, ring(): return lax.ppermute(value, axis, pairs)  1.81 us
  transfers between devices with their start and end apart: 5, of which 1 were waited for; matrix products, arithmetic and copies ran while one was open for 0% of the time, Pallas kernels for 5%

profile of v5, /device:TPU:1, one launch (start us, length us, event | category | flops | bytes accessed | tf_op | source)
XLA Modules:
  0.0 47.5 jit_solution(9976515134158803209)
XLA Ops:
  0.6 1.8 %shard_map.103 = (f32[19,8,8,128]{3,2,1,0:T(8,128)S(1)}, s32[64,128]{1,0:T(8,128)S(1)}, s32[2,1024]{1,0:T(2,128)S(1)}, f32[3,512]{1,0:T(4,128)S(1)}, f32[3,512]{...) custom-call(f32[19,8,8,128]{3,2,1,0:T(8,128)} %pop_in.1, ...), custom_call_target="tpu_custom_call" | custom-call | flops 1000000 | bytes 1048576 | tf_op jit(solution)/shard_map/pallas_call | solution.py:61
  2.4 11.5 %all-to-all-start = ((s32[128,1,128]{2,1,0:T(1,128)}), s32[128,1,128]{2,1,0:T(1,128)S(1)}, u32[]{:S(2)}, u32[]{:S(2)}) async-start(s32[128,1,128]{2,1,0:T(1,128)} %bitcast.4), calls=%async_computation | async-start | bytes 131072 | tf_op jit(solution)/shard_map/all_to_all | solution.py:583
  13.9 1.4 %collective-permute-start = (f32[56,128]{1,0:T(8,128)S(1)}, f32[56,128]{1,0:T(8,128)S(1)}, u32[]{:S(2)}, u32[]{:S(2)}) collective-permute-start(f32[56,128]{1,0:T(8,128)S(1)} %get-tuple-element.43), channel_id=1, source_target_pairs={{0,8},{8,16},{16,24},{24,32},{32,40},{40,48},{48,56},{56,64},{64,7... | collective-permute-start | bytes 86024 | tf_op jit(solution)/shard_map/ppermute | solution.py:571
  15.3 4.1 %collective-permute-start.1 = (f32[56,128]{1,0:T(8,128)S(1)}, f32[56,128]{1,0:T(8,128)S(1)}, u32[]{:S(2)}, u32[]{:S(2)}) collective-permute-start(f32[56,128]{1,0:T(8,128)S(1)} %get-tuple-element.44), channel_id=1, source_target_pairs={{8,0},{16,8},{24,16},{32,24},{40,32},{48,40},{56,48},{64,56},{72,6... | collective-permute-start | bytes 86024 | tf_op jit(solution)/shard_map/ppermute | solution.py:571
  19.5 1.8 %collective-permute-done.low = f32[56,128]{1,0:T(8,128)S(1)} collective-permute-done((f32[56,128]{1,0:T(8,128)S(1)}, f32[56,128]{1,0:T(8,128)S(1)}, u32[]{:S(2)}, u32[]{:S(2)}) %collective-permute-start) | collective-permute-done | bytes 28704 | tf_op jit(solution)/shard_map/ppermute | solution.py:571
  21.3 0.0 collective-permute-done.1.high
  21.3 1.1 %collective-permute-start.2 = (f32[64,128]{1,0:T(8,128)S(1)}, f32[64,128]{1,0:T(8,128)S(1)}, u32[]{:S(2)}, u32[]{:S(2)}) collective-permute-start(f32[64,128]{1,0:T(8,128)S(1)} %get-tuple-element.49), channel_id=1, source_target_pairs={{0,1},{1,0},{2,3},{3,2},{4,5},{5,4},{6,7},{7,6},{8,9},{9,8},{10,11... | collective-permute-start | bytes 98312 | tf_op jit(solution)/shard_map/ppermute | solution.py:579
  22.4 1.0 %collective-permute-start.3 = (f32[64,128]{1,0:T(8,128)S(1)}, f32[64,128]{1,0:T(8,128)S(1)}, u32[]{:S(2)}, u32[]{:S(2)}) collective-permute-start(f32[64,128]{1,0:T(8,128)S(1)} %get-tuple-element.53), channel_id=1, source_target_pairs={{1,2},{2,1},{3,4},{4,3},{5,6},{6,5},{7,0},{0,7},{9,10},{10,9},{11,... | collective-permute-start | bytes 98312 | tf_op jit(solution)/shard_map/ppermute | solution.py:579
  23.3 2.2 %shard_map.104 = (f32[1216,128]{1,0:T(8,128)S(1)}, f32[72,128]{1,0:T(8,128)S(1)}, bf16[128,2048]{1,0:T(8,128)(2,1)S(1)}, bf16[128,1024]{1,0:T(8,128)(2,1)S(1)}, f32[56,128]{1,0:T(8,128)S(1)}) custom-call(f32[1216,128]{1,0:T(8,128)S(1)} %get-tuple-element.39.g, f32[64,128]{1,0:T(8,128)S(1)} %get-tuple-element.40.r, f32[1216,128]{1,0:T(8,128)S(1)} %bitcast.11, ...), custom_call_target="tpu_custom_call" | custom-call | flops 1000000 | bytes 1048576 | tf_op jit(solution)/shard_map/pallas_call | solution.py:61
  25.6 0.0 collective-permute-done.2.y_one
  25.6 0.3 shard_map.106
  25.9 0.0 collective-permute-done.3.y_two
  25.9 0.0 all-to-all-done
  25.9 0.5 shard_map.107
  26.4 19.4 %all_to_all.16 = f32[128,2,128]{2,1,0:T(2,128)S(1)} all-to-all(f32[128,2,128]{2,1,0:T(2,128)S(1)} %bitcast.14), channel_id=1, replica_groups=mesh['gx'=16,'yz'=8] {'gx','yz'}, dimensions={0} | all-to-all | bytes 262144 | tf_op jit(solution)/shard_map/all_to_all | solution.py:583
  45.8 1.7 %shard_map.108 = (f32[1216,128]{1,0:T(8,128)}, f32[3,512]{1,0:T(4,128)}, f32[3,512]{1,0:T(4,128)}) custom-call(f32[256,128]{1,0:T(8,128)S(1)} %bitcast.12, s32[8,128]{1,0:T(8,128)S(1)} %get-tuple-element.56.rows_t, bf16[128,1024]{1,0:T(8,128)(2,1)S(1)} %get-tuple-element.57.hot, f32[1216,128]{1,0:T(8,128)S(1)} %get-tuple-element.58.base, ...), custom_call_target="tpu_custom_call" | custom-call | flops 1000000 | bytes 1048576 | tf_op jit(solution)/shard_map/pallas_call | solution.py:61
  (1 shorter events, 0.0 us)
Async XLA Ops:
  2.4 23.5 %all-to-all-start = ((s32[128,1,128]{2,1,0:T(1,128)}), s32[128,1,128]{2,1,0:T(1,128)S(1)}, u32[]{:S(2)}, u32[]{:S(2)}) async-start(s32[128,1,128]{2,1,0:T(1,128)} %bitcast.4), calls=%async_computation | async-start | bytes 131072 | tf_op jit(solution)/shard_map/all_to_all | solution.py:583
  13.9 7.3 %collective-permute-start = (f32[56,128]{1,0:T(8,128)S(1)}, f32[56,128]{1,0:T(8,128)S(1)}, u32[]{:S(2)}, u32[]{:S(2)}) collective-permute-start(f32[56,128]{1,0:T(8,128)S(1)} %get-tuple-element.43), channel_id=1, source_target_pairs={{0,8},{8,16},{16,24},{24,32},{32,40},{40,48},{48,56},{56,64},{64,7... | collective-permute-start | bytes 86024 | tf_op jit(solution)/shard_map/ppermute | solution.py:571
  15.3 5.9 %collective-permute-start.1 = (f32[56,128]{1,0:T(8,128)S(1)}, f32[56,128]{1,0:T(8,128)S(1)}, u32[]{:S(2)}, u32[]{:S(2)}) collective-permute-start(f32[56,128]{1,0:T(8,128)S(1)} %get-tuple-element.44), channel_id=1, source_target_pairs={{8,0},{16,8},{24,16},{32,24},{40,32},{48,40},{56,48},{64,56},{72,6... | collective-permute-start | bytes 86024 | tf_op jit(solution)/shard_map/ppermute | solution.py:571
  21.3 4.3 %collective-permute-start.2 = (f32[64,128]{1,0:T(8,128)S(1)}, f32[64,128]{1,0:T(8,128)S(1)}, u32[]{:S(2)}, u32[]{:S(2)}) collective-permute-start(f32[64,128]{1,0:T(8,128)S(1)} %get-tuple-element.49), channel_id=1, source_target_pairs={{0,1},{1,0},{2,3},{3,2},{4,5},{5,4},{6,7},{7,6},{8,9},{9,8},{10,11... | collective-permute-start | bytes 98312 | tf_op jit(solution)/shard_map/ppermute | solution.py:579
  22.4 3.5 %collective-permute-start.3 = (f32[64,128]{1,0:T(8,128)S(1)}, f32[64,128]{1,0:T(8,128)S(1)}, u32[]{:S(2)}, u32[]{:S(2)}) collective-permute-start(f32[64,128]{1,0:T(8,128)S(1)} %get-tuple-element.53), channel_id=1, source_target_pairs={{1,2},{2,1},{3,4},{4,3},{5,6},{6,5},{7,0},{0,7},{9,10},{10,9},{11,... | collective-permute-start | bytes 98312 | tf_op jit(solution)/shard_map/ppermute | solution.py:579
